TPU v7x, 32 devices: a whole 2x2x4 slice. The times are simulated.
32 devices in a mesh: grp: 2 (over core), row: 16 (over z, y, x).
Axes of the slice: x: 2, y: 2, z: 4, core: 2. Of those that a mesh axis runs over, the one named last changes fastest.
Arguments:
- block_tiles: bfloat16 [256, 2, 128, 128], P(('grp', 'row')), may hold values from -4 to 4
- tile_columns: int32 [256, 2], replicated, may hold values from -1 to 255, as said below
- requests: int32 [32, 32], P(('grp', 'row')), may hold values from -1 to 7, as said below
- output_columns: int32 [256, 2], P(('grp', 'row')), may hold values from 0 to 255, as said below
Outputs:
- product_tiles: bfloat16 [256, 2, 128, 128], P(('grp', 'row'))
Inputs may be any that keep to these rules, and one draw needn't show every extreme that they name: `tile_columns`: every block-row has 1 to 2 present tiles (entries >= 0) with different block columns; the data of absent tiles are never read. One device's present tiles number at most 14, exactly 14 on some device in every draw, and name 10 different block columns, at most one block-row of each owner. requests[d, e] is the local index of the block-row of owner e that device d's present tiles name, or -1 where they name none. `output_columns`: the 2 block columns of one block-row differ.
All inputs are finite; a program needn't handle non-finite values.
Results may differ from a plain program's by a relative error of at most 0.001.
Values may be sent and summed in bfloat16 or wider, within the bound.
A program may use at most 128 MiB of HBM per device.

v0:
```python
import functools

import jax
import jax.numpy as jnp
from jax import lax
from jax.experimental import pallas as pl
from jax.experimental.pallas import tpu as pltpu
from jax.sharding import PartitionSpec as P

MESH = pl.DeviceIdType.MESH


def multiply(base, find, cols_ref, outs_ref, tiles_ref, rbuf, out_ref):
    rows, per_row, side, _ = tiles_ref.shape
    outs_row = outs_ref.shape[0]
    for i in range(rows):
        left = jnp.concatenate([tiles_ref[i, k] for k in range(per_row)], axis=1)
        stack = []
        for k in range(per_row):
            c = cols_ref[k, base + i]
            safe = jnp.maximum(c, 0)
            slot = find(safe // rows)
            line = []
            for p in range(outs_row):
                o = outs_ref[p, i]
                which = jnp.int32(0)
                hit = jnp.int32(0)
                for j in range(per_row):
                    same = cols_ref[j, safe] == o
                    which = jnp.where(same, j, which)
                    hit = jnp.where(same & (c >= 0), 1, hit)
                tile = rbuf[slot, which]
                line.append(tile * hit.astype(jnp.float32).astype(jnp.bfloat16))
            stack.append(jnp.concatenate(line, axis=1))
        right = jnp.concatenate(stack, axis=0)
        prod = jnp.dot(left, right, preferred_element_type=jnp.float32).astype(jnp.bfloat16)
        for p in range(outs_row):
            out_ref[i, p] = prod[:, p * side : (p + 1) * side]


def dense_kernel(
    groups, members, cols_ref, outs_ref, tiles_ref, out_ref,
    sbuf, rbuf, mbuf, send_sem, recv_sem, mirror_send, mirror_recv,
):
    part = members // 2
    n = groups * part
    rows, per_row, side, _ = tiles_ref.shape
    grp, row = lax.axis_index("grp"), lax.axis_index("row")
    half, spot = row // part, lax.rem(row, part)
    me = grp * part + spot
    base = (grp * members + row) * rows
    mirror_row = (1 - half) * part + spot
    mirror = {"grp": grp, "row": mirror_row}
    mirror_base = (grp * members + mirror_row) * rows

    def place(s):
        u = lax.rem(me + s, n)
        return u // part, half * part + lax.rem(u, part)

    def target(s):
        g, r = place(s)
        return {"grp": g, "row": r}

    barrier = pltpu.get_barrier_semaphore()
    pl.semaphore_signal(barrier, inc=1, device_id=mirror, device_id_type=MESH)

    def greet(s, carry):
        pl.semaphore_signal(barrier, inc=1, device_id=target(s), device_id_type=MESH)
        return carry

    lax.fori_loop(1, n, greet, 0)

    def asked(s, start):
        g, r = place(s)
        first = (g * members + r) * rows
        t = jnp.int32(0)
        for i in range(rows):
            for k in range(per_row):
                c = cols_ref[k, first + i] - start
                t = jnp.where((c >= 0) & (c < rows), c, t)
        return t

    def copy(s, level):
        return pltpu.make_async_remote_copy(
            src_ref=sbuf.at[level * n + s],
            dst_ref=rbuf.at[level * n + s],
            send_sem=send_sem.at[level * n + s],
            recv_sem=recv_sem.at[level * n + s],
            device_id=target(s),
            device_id_type=MESH,
        )

    def pack(s, carry):
        sbuf[s] = tiles_ref[asked(s, base)]
        return carry

    lax.fori_loop(1, n, pack, 0)
    pl.semaphore_wait(barrier, n)
    across = pltpu.make_async_remote_copy(
        src_ref=tiles_ref,
        dst_ref=mbuf,
        send_sem=mirror_send,
        recv_sem=mirror_recv,
        device_id=mirror,
        device_id_type=MESH,
    )
    across.start()

    def send(s, carry):
        copy(s, 0).start()
        return carry

    lax.fori_loop(1, n, send, 0)
    rbuf[0] = tiles_ref[asked(0, base)]
    across.wait()

    def relay(s, carry):
        sbuf[n + s] = mbuf[asked(s, mirror_base)]
        return carry

    lax.fori_loop(1, n, relay, 0)

    def forward(s, carry):
        copy(s, 1).start()
        return carry

    lax.fori_loop(1, n, forward, 0)
    rbuf[n] = mbuf[asked(0, mirror_base)]

    def land(s, carry):
        copy(s, 0).wait()
        copy(s, 1).wait()
        return carry

    lax.fori_loop(1, n, land, 0)

    def find(owner):
        owner_row = lax.rem(owner, members)
        spot_of = owner // members * part + lax.rem(owner_row, part)
        return lax.rem(me - spot_of + n, n) + jnp.where(owner_row // part == half, 0, n)

    multiply(base, find, cols_ref, outs_ref, tiles_ref, rbuf, out_ref)


def row_mask(cols_ref, groups, members, first_row, count, start, rows):
    mask = jnp.int32(0)
    for g in range(groups):

        def look(x, mask):
            for i in range(rows):
                for k in range(cols_ref.shape[0]):
                    c = cols_ref[k, (g * members + first_row + x) * rows + i] - start
                    bit = jnp.left_shift(jnp.int32(1), jnp.clip(c, 0, rows - 1))
                    mask = mask | jnp.where((c >= 0) & (c < rows), bit, 0)
            return mask

        mask = lax.fori_loop(0, count, look, mask)
    return mask


def rank(mask, t, rows, slots):
    total = jnp.int32(0)
    for i in range(rows):
        total += jnp.where(i < t, jnp.right_shift(mask, i) & 1, 0)
    return jnp.minimum(total, slots - 1)


def nth(mask, q, rows):
    seen = jnp.int32(0)
    found = jnp.int32(0)
    for i in range(rows):
        bit = jnp.right_shift(mask, i) & 1
        found = jnp.where((bit == 1) & (seen == q), i, found)
        seen += bit
    return found


def overflow(cols_ref, groups, members, rows, half_slots):
    part = members // 2
    total = groups * members * rows
    lines = -(-total // 1024) * 8
    index = lax.broadcasted_iota(jnp.int32, (lines, 128), 0) * 128
    index = index + lax.broadcasted_iota(jnp.int32, (lines, 128), 1)
    hits = []
    for q in range(2):
        hit = jnp.zeros((lines, 128), jnp.int32)
        for g in range(groups):

            def look(x, hit):
                for i in range(rows):
                    for k in range(cols_ref.shape[0]):
                        c = cols_ref[k, (g * members + q * part + x) * rows + i]
                        hit = jnp.where(index == c, 1, hit)
                return hit

            hit = lax.fori_loop(0, part, look, hit)
        hits.append(hit)
    far = jnp.where(lax.rem(index // rows, members) < part, hits[1], hits[0])
    lane_in = lax.broadcasted_iota(jnp.int32, (128, 128), 0) // rows
    lane_out = lax.broadcasted_iota(jnp.int32, (128, 128), 1) // rows
    blocks = jnp.where(lane_in == lane_out, 1.0, 0.0).astype(jnp.bfloat16)
    ones = far.astype(jnp.float32).astype(jnp.bfloat16)
    count = jnp.dot(ones, blocks, preferred_element_type=jnp.float32)
    return jnp.max(count - half_slots).astype(jnp.int32)


def compact_kernel(
    groups, members, half_slots, cols_ref, outs_ref, tiles_ref, out_ref, over_ref,
    sbuf, rbuf, far_out, far_in, slot_ref, send_sem, recv_sem, side_send, side_recv,
):
    part = members // 2
    n = groups * part
    rows, per_row, side, _ = tiles_ref.shape
    grp, row = lax.axis_index("grp"), lax.axis_index("row")
    half, spot = row // part, lax.rem(row, part)
    me = grp * part + spot
    base = (grp * members + row) * rows
    far_row = (1 - half) * part + spot
    far = {"grp": grp, "row": far_row}
    far_base = (grp * members + far_row) * rows
    def in_half(s):
        u = lax.rem(me + s, n)
        return u // part, half * part + lax.rem(u, part)

    def device(spot_of):
        g, r = spot_of
        return {"grp": g, "row": r}

    barrier = pltpu.get_barrier_semaphore()
    pl.semaphore_signal(barrier, inc=1, device_id=far, device_id_type=MESH)

    def greet(s, carry):
        pl.semaphore_signal(barrier, inc=1, device_id=device(in_half(s)), device_id_type=MESH)
        return carry

    lax.fori_loop(1, n, greet, 0)

    def asked(spot_of, start):
        g, r = spot_of
        first = (g * members + r) * rows
        t = jnp.int32(0)
        for i in range(rows):
            for k in range(per_row):
                c = cols_ref[k, first + i] - start
                t = jnp.where((c >= 0) & (c < rows), c, t)
        return t

    def mask_of(first_row, count, start):
        return row_mask(cols_ref, groups, members, first_row, count, start, rows)

    def copy(slot, where):
        return pltpu.make_async_remote_copy(
            src_ref=sbuf.at[slot],
            dst_ref=rbuf.at[slot],
            send_sem=send_sem.at[slot],
            recv_sem=recv_sem.at[slot],
            device_id=device(where),
            device_id_type=MESH,
        )

    far_mask = mask_of((1 - half) * part, part, base)
    for q in range(half_slots):
        far_out[q] = tiles_ref[nth(far_mask, q, rows)]
    def pack(s, carry):
        sbuf[s] = tiles_ref[asked(in_half(s), base)]
        return carry

    lax.fori_loop(1, n, pack, 0)
    pl.semaphore_wait(barrier, n)
    across = pltpu.make_async_remote_copy(
        src_ref=far_out, dst_ref=far_in, send_sem=side_send, recv_sem=side_recv,
        device_id=far, device_id_type=MESH,
    )
    across.start()
    def send(s, carry):
        copy(s, in_half(s)).start()
        return carry

    lax.fori_loop(1, n, send, 0)
    rbuf[0] = tiles_ref[asked(in_half(0), base)]
    over_ref[0] = overflow(cols_ref, groups, members, rows, half_slots)
    far_mask_in = mask_of(half * part, part, far_base)
    def slot_far(s, carry):
        t = asked(in_half(s), far_base)
        slot_ref[s] = rank(far_mask_in, t, rows, half_slots)
        return carry

    lax.fori_loop(0, n, slot_far, 0)
    across.wait()

    def relay_far(s, carry):
        sbuf[n + s] = far_in[slot_ref[s]]
        return carry

    lax.fori_loop(1, n, relay_far, 0)

    def forward_far(s, carry):
        copy(n + s, in_half(s)).start()
        return carry

    lax.fori_loop(1, n, forward_far, 0)
    rbuf[n] = far_in[slot_ref[0]]

    def land_half(s, carry):
        copy(s, in_half(s)).wait()
        copy(n + s, in_half(s)).wait()
        return carry

    lax.fori_loop(1, n, land_half, 0)

    def find(owner):
        g, r = owner // members, lax.rem(owner, members)
        slot = lax.rem(me - g * part - lax.rem(r, part) + n, n)
        return slot + jnp.where(r // part == half, 0, n)

    multiply(base, find, cols_ref, outs_ref, tiles_ref, rbuf, out_ref)


def params(identity):
    return pltpu.CompilerParams(
        collective_id=identity, has_side_effects=True, vmem_limit_bytes=56 * 1024 * 1024
    )


def shards(block_tiles, tile_columns, requests, output_columns):
    groups = lax.axis_size("grp")
    members = lax.axis_size("row")
    n = groups * members
    half = n // 2
    rows, per_row, side, _ = block_tiles.shape
    vmem = pl.BlockSpec(memory_space=pltpu.VMEM)
    smem = pl.BlockSpec(memory_space=pltpu.SMEM)
    out = jax.ShapeDtypeStruct((rows, output_columns.shape[1], side, side), jnp.bfloat16)
    tile_rows = lambda count: pltpu.VMEM((count, per_row, side, side), jnp.bfloat16)
    operands = (tile_columns.T, output_columns.T, block_tiles)

    def dense():
        return pl.pallas_call(
            functools.partial(dense_kernel, groups, members),
            out_shape=out,
            in_specs=[smem, smem, vmem],
            out_specs=vmem,
            scratch_shapes=[
                tile_rows(n),
                tile_rows(n),
                tile_rows(rows),
                pltpu.SemaphoreType.DMA((n,)),
                pltpu.SemaphoreType.DMA((n,)),
                pltpu.SemaphoreType.DMA,
                pltpu.SemaphoreType.DMA,
            ],
            compiler_params=params(0),
        )(*operands)

    if half > 2 * rows:
        return dense()
    half_slots = rows * 3 // 4
    compact, over = pl.pallas_call(
        functools.partial(compact_kernel, groups, members, half_slots),
        out_shape=(out, jax.ShapeDtypeStruct((1,), jnp.int32)),
        in_specs=[smem, smem, vmem],
        out_specs=(vmem, smem),
        scratch_shapes=[
            tile_rows(n),
            tile_rows(n),
            tile_rows(half_slots),
            tile_rows(half_slots),
            pltpu.SMEM((half,), jnp.int32),
            pltpu.SemaphoreType.DMA((n,)),
            pltpu.SemaphoreType.DMA((n,)),
            pltpu.SemaphoreType.DMA,
            pltpu.SemaphoreType.DMA,
        ],
        compiler_params=params(1),
    )(*operands)
    return lax.cond(over[0] > 0, dense, lambda: compact)


def solution(mesh):
    placed = (
        P(("grp", "row"), None, None, None),
        P(),
        P(("grp", "row"), None),
        P(("grp", "row"), None),
    )
    return jax.shard_map(
        shards,
        mesh=mesh,
        in_specs=placed,
        out_specs=P(("grp", "row"), None, None, None),
        check_vma=False,
    )
```

profile of v0, /device:TPU:0, one launch (start us, length us, event | category | flops | bytes accessed | tf_op | source)
XLA Modules:
  0.0 43.2 jit_solution(1183256523769170904)
XLA Ops:
  0.0 0.0 copy-start
  0.0 41.2 %shard_map.39 = (bf16[8,2,128,128]{3,2,1,0:T(8,128)(2,1)S(1)}, s32[1]{0:T(128)}) custom-call(s32[2,256]{1,0:T(2,128)} %bitcast.3, s32[2,8]{1,0:T(2,128)} %bitcast.5, bf16[8,2,128,128]{3,2,1,0:T(8,128)(2,1)} %tiles_ref.1), custom_call_target="tpu_custom_call" | custom-call | tf_op jit(solution)/shard_map/pallas_call | solution.py:358
  41.7 0.0 copy-start.1
  41.7 0.0 copy-start.2
  41.7 0.0 copy-done
  41.8 0.7 %copy-done.1 = s32[256,2]{0,1:T(2,128)S(1)} copy-done((s32[256,2]{0,1:T(2,128)S(1)}, s32[256,2]{0,1:T(2,128)}, u32[]{:S(2)}) %copy-start.1) | copy-done | bytes 2072
  42.4 0.0 copy-done.2
  42.4 0.8 %copy.9 = bf16[8,2,128,128]{3,2,1,0:T(8,128)(2,1)} copy(bf16[8,2,128,128]{3,2,1,0:T(8,128)(2,1)S(1)} %get-tuple-element.22) | data formatting | bytes 1048576
  (1 shorter events, 0.0 us)
Async XLA Ops:
  0.0 41.7 %copy-start = (bf16[8,2,128,128]{3,2,1,0:T(8,128)(2,1)S(1)}, bf16[8,2,128,128]{3,2,1,0:T(8,128)(2,1)}, u32[]{:S(2)}) copy-start(bf16[8,2,128,128]{3,2,1,0:T(8,128)(2,1)} %tiles_ref.1) | copy-start | bytes 1572868
  41.7 0.7 %copy-start.1 = (s32[256,2]{0,1:T(2,128)S(1)}, s32[256,2]{0,1:T(2,128)}, u32[]{:S(2)}) copy-start(s32[256,2]{0,1:T(2,128)} %param.7) | copy-start | bytes 6148
  41.7 0.7 %copy-start.2 = (s32[8,2]{0,1:T(2,128)S(1)}, s32[8,2]{0,1:T(2,128)}, u32[]{:S(2)}) copy-start(s32[8,2]{0,1:T(2,128)} %param.8) | copy-start | bytes 196
where the time goes:
time: 43.4 us; the launch traced here: 43.2 us
  Pallas kernels  41.2 us (95%)
  local copies, waits for them, and re-layouts  1.47 us (3%)
  between operations  0.59 us (1%)
    pallas_call x1, Pallas kernels, shards(): pl.pallas_call(functools.partial(compact_kernel, groups, members, half_sl...  41.2 us
    unnamed x7, local copies, waits for them, and re-layouts  1.47 us

commit v1 on v0

v1 whole, which is shorter than its diff:
```python
import functools

import jax
import jax.numpy as jnp
from jax import lax
from jax.experimental import pallas as pl
from jax.experimental.pallas import tpu as pltpu
from jax.sharding import PartitionSpec as P

MESH = pl.DeviceIdType.MESH
PLANE = 4
CUT_B = (4, 18)
CAP_B = 32
CUT_C = (4,)
CAP_C = 21


def multiply(base, find, cols_ref, outs_ref, tiles_ref, rbuf, out_ref):
    rows, per_row, side, _ = tiles_ref.shape
    outs_row = outs_ref.shape[0]
    for i in range(rows):
        left = jnp.concatenate([tiles_ref[i, k] for k in range(per_row)], axis=1)
        stack = []
        for k in range(per_row):
            c = cols_ref[k, base + i]
            safe = jnp.maximum(c, 0)
            slot = find(safe // rows)
            line = []
            for p in range(outs_row):
                o = outs_ref[p, i]
                which = jnp.int32(0)
                hit = jnp.int32(0)
                for j in range(per_row):
                    same = cols_ref[j, safe] == o
                    which = jnp.where(same, j, which)
                    hit = jnp.where(same & (c >= 0), 1, hit)
                tile = rbuf[slot, which]
                line.append(tile * hit.astype(jnp.float32).astype(jnp.bfloat16))
            stack.append(jnp.concatenate(line, axis=1))
        right = jnp.concatenate(stack, axis=0)
        prod = jnp.dot(left, right, preferred_element_type=jnp.float32).astype(jnp.bfloat16)
        for p in range(outs_row):
            out_ref[i, p] = prod[:, p * side : (p + 1) * side]


def dense_kernel(
    groups, members, cols_ref, outs_ref, tiles_ref, out_ref,
    sbuf, rbuf, mbuf, send_sem, recv_sem, mirror_send, mirror_recv,
):
    part = members // 2
    n = groups * part
    rows, per_row, side, _ = tiles_ref.shape
    grp, row = lax.axis_index("grp"), lax.axis_index("row")
    half, spot = row // part, lax.rem(row, part)
    me = grp * part + spot
    base = (grp * members + row) * rows
    mirror_row = (1 - half) * part + spot
    mirror = {"grp": grp, "row": mirror_row}
    mirror_base = (grp * members + mirror_row) * rows

    def place(s):
        u = lax.rem(me + s, n)
        return u // part, half * part + lax.rem(u, part)

    def target(s):
        g, r = place(s)
        return {"grp": g, "row": r}

    barrier = pltpu.get_barrier_semaphore()
    pl.semaphore_signal(barrier, inc=1, device_id=mirror, device_id_type=MESH)

    def greet(s, carry):
        pl.semaphore_signal(barrier, inc=1, device_id=target(s), device_id_type=MESH)
        return carry

    lax.fori_loop(1, n, greet, 0)

    def asked(s, start):
        g, r = place(s)
        first = (g * members + r) * rows
        t = jnp.int32(0)
        for i in range(rows):
            for k in range(per_row):
                c = cols_ref[k, first + i] - start
                t = jnp.where((c >= 0) & (c < rows), c, t)
        return t

    def copy(s, level):
        return pltpu.make_async_remote_copy(
            src_ref=sbuf.at[level * n + s],
            dst_ref=rbuf.at[level * n + s],
            send_sem=send_sem.at[level * n + s],
            recv_sem=recv_sem.at[level * n + s],
            device_id=target(s),
            device_id_type=MESH,
        )

    def pack(s, carry):
        sbuf[s] = tiles_ref[asked(s, base)]
        return carry

    lax.fori_loop(1, n, pack, 0)
    pl.semaphore_wait(barrier, n)
    across = pltpu.make_async_remote_copy(
        src_ref=tiles_ref,
        dst_ref=mbuf,
        send_sem=mirror_send,
        recv_sem=mirror_recv,
        device_id=mirror,
        device_id_type=MESH,
    )
    across.start()

    def send(s, carry):
        copy(s, 0).start()
        return carry

    lax.fori_loop(1, n, send, 0)
    rbuf[0] = tiles_ref[asked(0, base)]
    across.wait()

    def relay(s, carry):
        sbuf[n + s] = mbuf[asked(s, mirror_base)]
        return carry

    lax.fori_loop(1, n, relay, 0)

    def forward(s, carry):
        copy(s, 1).start()
        return carry

    lax.fori_loop(1, n, forward, 0)
    rbuf[n] = mbuf[asked(0, mirror_base)]

    def land(s, carry):
        copy(s, 0).wait()
        copy(s, 1).wait()
        return carry

    lax.fori_loop(1, n, land, 0)

    def find(owner):
        owner_row = lax.rem(owner, members)
        spot_of = owner // members * part + lax.rem(owner_row, part)
        return lax.rem(me - spot_of + n, n) + jnp.where(owner_row // part == half, 0, n)

    multiply(base, find, cols_ref, outs_ref, tiles_ref, rbuf, out_ref)


def same(lane, rows, groups, members):
    device = lane // rows
    inner = lax.rem(device, members)
    spot = lax.rem(inner, PLANE)
    return device // members, inner // PLANE, spot // 2, lax.rem(spot, 2)


def level(rel):
    spot = lax.rem(rel, PLANE)
    return jnp.where(spot == 0, 0, jnp.where(spot == PLANE - 1, 2, 1))


def ones(mask):
    return jnp.where(mask, 1.0, 0.0)


def across(a, b):
    dims = (((1,), (1,)), ((), ()))
    return lax.dot_general(
        a.astype(jnp.bfloat16), b.astype(jnp.bfloat16), dims, preferred_element_type=jnp.float32
    )


def iota(shape, axis):
    return lax.broadcasted_iota(jnp.int32, shape, axis)


def named_rows(cols, here, rows, groups, members):
    g, z, y, x = here
    lines = members // PLANE
    total = cols.shape[1]
    devices = groups * members
    count = devices + 16
    query = iota((count, total), 0)
    lane = iota((count, total), 1)
    og, oz, oy, ox = same(lane, rows, groups, members)
    rel = PLANE * lax.rem(og + g, 2) + 2 * lax.rem(oy + y, 2) + lax.rem(ox + x, 2)
    step = query - devices
    alone = (step < 0) & (lane // rows == query)
    plane = (step >= 0) & (step < lines) & (oz == lax.rem(z + jnp.maximum(step, 0), lines))
    near = (oz == z) & (rel == step - 8)
    group = ones(alone | plane | near)
    index = iota((total, total), 0)
    hits = jnp.zeros((count, total), jnp.float32)
    for k in range(cols.shape[0]):
        hits = hits + across(group, ones(index == cols[k : k + 1]))
    return ones(hits > 0.5)


def tables(cols, named, here, rows, groups, members):
    g, z, y, x = here
    lines = members // PLANE
    devices = groups * members
    total = cols.shape[1]
    per = cols.shape[0]
    lane = iota((8, total), 1)
    sub = iota((8, total), 0)
    og, oz, oy, ox = same(lane, rows, groups, members)
    rel = PLANE * lax.rem(og + g, 2) + 2 * lax.rem(oy + y, 2) + lax.rem(ox + x, 2)
    lev = level(rel)
    local = oz == z
    back = lax.rem(z - oz + lines, lines)
    planes = named[devices : devices + 8]
    mine = jnp.broadcast_to(planes[0:1], (8, total))
    near = named[devices + 8 : devices + 16]
    sends = [planes * ones(local & (lev == k)) for k in range(3)]
    takes = [mine * ones((back == sub) & (lev == k)) for k in range(3)]
    mids = [near * ones(local), near * ones(~local)]
    stack = jnp.concatenate(sends + takes + mids, axis=0)
    upper = ones(iota((total, total), 0) > iota((total, total), 1))
    masks, ranks = [], []
    before = jnp.zeros((stack.shape[0], 1), jnp.float32)
    for j in range(per):
        m = stack * ones(cols[j : j + 1] >= 0)
        ranks.append(across(m, upper) + before)
        masks.append(m)
        before = before + jnp.sum(m, axis=1, keepdims=True)

    def slots(first, bounds):
        parts = range(first, first + len(bounds))
        sums = [before[8 * b : 8 * b + 8] for b in parts]
        start = jnp.zeros((8, 1), jnp.float32)
        where = []
        used = [jnp.zeros((8, total), jnp.float32) for j in range(per)]
        at = [jnp.zeros((8, total), jnp.float32) for j in range(per)]
        for b, bound, n in zip(parts, bounds, sums):
            start = jnp.maximum(start, bound)
            for j in range(per):
                m = masks[j][8 * b : 8 * b + 8]
                used[j] = used[j] + m
                at[j] = at[j] + m * (start + ranks[j][8 * b : 8 * b + 8])
            start = start + n
        return used, at

    send_used, send_at = slots(0, (0.0, CUT_B[0], CUT_B[1]))
    take_used, take_at = slots(3, (0.0, CUT_B[0], CUT_B[1]))
    mid_used, mid_at = slots(6, (0.0, CUT_C[0]))
    item = lax.rem(lane, rows)
    held = groups * PLANE * rows * per
    home = [(rel * (rows * per) + item * per + j).astype(jnp.float32) for j in range(per)]
    offset = (held + (sub - 1) * CAP_B).astype(jnp.float32)
    arrived = []
    for j in range(per):
        far = jnp.sum(take_used[j] * (offset + jnp.minimum(take_at[j], CAP_B - 1.0)), axis=0, keepdims=True)
        arrived.append(jnp.where(local, home[j], jnp.broadcast_to(far, (8, total))))

    def sources(used, at, address, first, count):
        out = jnp.zeros((8, 32 * count), jnp.float32)
        slot = iota((32, total), 0)
        for j in range(per):
            spot = jnp.where(used[j] > 0.5, at[j], -1.0).astype(jnp.int32)
            hot = jnp.concatenate(
                [ones(slot == spot[first + q : first + q + 1]) for q in range(count)], axis=0
            )
            out = out + across(address[j], hot)
        return jnp.clip(out.astype(jnp.int32), 0, held + (lines - 1) * CAP_B - 1)

    b_list = sources(send_used, send_at, home, 0, lines)
    c_list = sources(mid_used, mid_at, arrived, 0, groups * PLANE)
    final = [jnp.clip(mid_at[j][0:1].astype(jnp.int32), 0, CAP_C - 1) for j in range(per)]
    lines_out = [b_list[0:1, :128], c_list[0:1, :128], c_list[0:1, 128:256]]
    for j in range(per):
        for h in range(total // 128):
            lines_out.append(final[j][:, 128 * h : 128 * h + 128])
    lines_out.append(jnp.zeros((1, 128), jnp.int32))
    return jnp.concatenate(lines_out, axis=0)


def overflow(cols, named, here, rows, groups, members):
    g, z, y, x = here
    lines = members // PLANE
    devices = groups * members
    total = cols.shape[1]
    count = sum(ones(cols[j : j + 1] >= 0) for j in range(cols.shape[0]))
    lane = iota((devices, total), 1)
    row = iota((devices, total), 0)
    local = lax.rem(row, members) // PLANE == lax.rem(lane // rows, members) // PLANE
    load = named[:devices] * count
    inner = jnp.sum(load * ones(local), axis=1, keepdims=True)
    outer = jnp.sum(load * ones(~local), axis=1, keepdims=True)
    over = jnp.max(jnp.maximum(inner, CUT_C[0]) + outer - CAP_C)
    owner = ones(iota((128, total), 0) == iota((128, total), 1) // rows)
    by_owner = across(named[devices : devices + 8] * count, owner)
    at = iota((128, 128), 0)
    of = iota((128, 128), 1)
    ag, az, ay, ax = same(at, 1, groups, members)
    og, oz, oy, ox = same(of, 1, groups, members)
    rel = PLANE * lax.rem(og + ag, 2) + 2 * lax.rem(oy + ay, 2) + lax.rem(ox + ax, 2)
    valid = (az == oz) & (at < devices) & (of < devices)
    start = jnp.zeros((8, 128), jnp.float32)
    for k, bound in enumerate((0.0, CUT_B[0], CUT_B[1])):
        start = jnp.maximum(start, bound)
        start = start + across(by_owner, ones(valid & (level(rel) == k)))
    sub = iota((8, 128), 0)
    source = lax.rem(iota((8, 128), 1), members) // PLANE
    counted = (sub < lines) & (source != lax.rem(z + sub, lines))
    return jnp.maximum(over, jnp.max(jnp.where(counted, start - CAP_B, 0.0))).astype(jnp.int32)


def compact_kernel(
    groups, members, cols_ref, outs_ref, cols_vec, tiles_hbm, out_ref, over_ref,
    tiles, parts, arena, b_send, b_recv, c_send, c_recv, tab_vec, tab,
    load_sem, tab_sem, a_out, a_in, b_out, b_in, c_out, c_in,
):
    rows, per, side, _ = tiles.shape
    lines = members // PLANE
    crowd = groups * PLANE
    piece = side // crowd
    g, row = lax.axis_index("grp"), lax.axis_index("row")
    z, spot = row // PLANE, lax.rem(row, PLANE)
    y, x = spot // 2, lax.rem(spot, 2)
    here = (g, z, y, x)
    base = (g * members + row) * rows
    me = g * PLANE + spot

    def near(u):
        dg, dy, dx = u // PLANE, u // 2 % 2, u % 2
        return lax.rem(g + dg, 2), 2 * lax.rem(y + dy, 2) + lax.rem(x + dx, 2)

    def near_device(u):
        ng, ns = near(u)
        return {"grp": ng, "row": z * PLANE + ns}

    def line_device(dz):
        return {"grp": g, "row": lax.rem(z + dz, lines) * PLANE + spot}

    load = pltpu.make_async_copy(tiles_hbm, tiles, load_sem)
    load.start()
    barrier = pltpu.get_barrier_semaphore()
    for dz in range(1, lines):
        pl.semaphore_signal(barrier, inc=1, device_id=line_device(dz), device_id_type=MESH)
    for u in range(1, crowd):
        pl.semaphore_signal(barrier, inc=1, device_id=near_device(u), device_id_type=MESH)

    cols = cols_vec[...]
    named = named_rows(cols, here, rows, groups, members)
    tab_vec[...] = tables(cols, named, here, rows, groups, members)
    move = pltpu.make_async_copy(tab_vec, tab, tab_sem)
    move.start()
    load.wait()
    pl.semaphore_wait(barrier, lines - 1 + crowd - 1)

    def a_copy(u):
        ng, ns = near(u)
        start = pl.multiple_of((ng * PLANE + ns) * piece, piece)
        return pltpu.make_async_remote_copy(
            src_ref=tiles.at[:, :, pl.ds(start, piece), :],
            dst_ref=parts.at[u],
            send_sem=a_out.at[u],
            recv_sem=a_in.at[u],
            device_id=near_device(u),
            device_id_type=MESH,
        )

    order = [4, 1, 2, 5, 6, 3, 7]
    for u in order:
        a_copy(u).start()

    def settle(u):
        for i in range(rows):
            for j in range(per):
                arena[(u * rows + i) * per + j] = parts[u, i, j]

    mine = pl.multiple_of(me * piece, piece)
    for i in range(rows):
        for j in range(per):
            arena[i * per + j] = tiles[i, j, pl.ds(mine, piece), :]
    move.wait()

    cuts_b = (0,) + CUT_B + (CAP_B,)
    cuts_c = (0,) + CUT_C + (CAP_C,)

    def b_copy(k, dz):
        span = pl.ds(cuts_b[k], cuts_b[k + 1] - cuts_b[k])
        return pltpu.make_async_remote_copy(
            src_ref=b_send.at[dz - 1, span],
            dst_ref=b_recv.at[dz - 1, span],
            send_sem=b_out.at[3 * (dz - 1) + k],
            recv_sem=b_in.at[3 * (dz - 1) + k],
            device_id=line_device(dz),
            device_id_type=MESH,
        )

    def c_copy(k, u):
        span = pl.ds(cuts_c[k], cuts_c[k + 1] - cuts_c[k])
        return pltpu.make_async_remote_copy(
            src_ref=c_send.at[u, span],
            dst_ref=c_recv.at[u, span],
            send_sem=c_out.at[2 * u + k],
            recv_sem=c_in.at[2 * u + k],
            device_id=near_device(u),
            device_id_type=MESH,
        )

    def push_b(k):
        for dz in range(1, lines):
            for q in range(cuts_b[k], cuts_b[k + 1]):
                b_send[dz - 1, q] = arena[tab[0, 32 * dz + q]]
            b_copy(k, dz).start()

    def push_c(k):
        for u in order + [0]:
            for q in range(cuts_c[k], cuts_c[k + 1]):
                tile = arena[tab[1 + u // 4, 32 * (u % 4) + q]]
                if u:
                    c_send[u, q] = tile
                else:
                    c_recv[0, q] = tile
            if u:
                c_copy(k, u).start()

    a_copy(4).wait_recv()
    settle(4)
    push_b(0)
    over_ref[0] = overflow(cols, named, here, rows, groups, members)
    for u in (1, 2, 5, 6):
        a_copy(u).wait_recv()
        settle(u)
    push_b(1)
    for u in (3, 7):
        a_copy(u).wait_recv()
        settle(u)
    push_b(2)
    push_c(0)
    held = crowd * rows * per
    for k in range(3):
        for dz in range(1, lines):
            b_copy(k, dz).wait_recv()
            for q in range(cuts_b[k], cuts_b[k + 1]):
                arena[held + (dz - 1) * CAP_B + q] = b_recv[dz - 1, q]
    push_c(1)

    sources = []
    for piece_of in range(crowd):
        pg, ps = piece_of // PLANE, piece_of % PLANE
        dy, dx = lax.rem(ps // 2 + y, 2), lax.rem(ps % 2 + x, 2)
        sources.append(PLANE * lax.rem(pg + g, 2) + 2 * dy + dx)
    for u in range(1, crowd):
        for k in range(2):
            c_copy(k, u).wait_recv()

    outs_row = outs_ref.shape[0]
    wide = cols_ref.shape[1] // 128
    for i in range(rows):
        left = jnp.concatenate([tiles[i, k] for k in range(per)], axis=1)
        stack = []
        for k in range(per):
            c = cols_ref[k, base + i]
            safe = jnp.maximum(c, 0)
            line = []
            for p in range(outs_row):
                o = outs_ref[p, i]
                which = jnp.int32(0)
                hit = jnp.int32(0)
                for j in range(per):
                    match = cols_ref[j, safe] == o
                    which = jnp.where(match, j, which)
                    hit = jnp.where(match & (c >= 0), 1, hit)
                slot = tab[3 + wide * which + safe // 128, lax.rem(safe, 128)]
                tile = jnp.concatenate([c_recv[s, slot] for s in sources], axis=0)
                line.append(tile * hit.astype(jnp.float32).astype(jnp.bfloat16))
            stack.append(jnp.concatenate(line, axis=1))
        right = jnp.concatenate(stack, axis=0)
        prod = jnp.dot(left, right, preferred_element_type=jnp.float32).astype(jnp.bfloat16)
        for p in range(outs_row):
            out_ref[i, p] = prod[:, p * side : (p + 1) * side]

    for u in range(1, crowd):
        a_copy(u).wait_send()
        for k in range(2):
            c_copy(k, u).wait_send()
    for dz in range(1, lines):
        for k in range(3):
            b_copy(k, dz).wait_send()


def params(identity):
    return pltpu.CompilerParams(
        collective_id=identity, has_side_effects=True, vmem_limit_bytes=56 * 1024 * 1024
    )


def shards(block_tiles, tile_columns, requests, output_columns):
    groups = lax.axis_size("grp")
    members = lax.axis_size("row")
    n = groups * members
    rows, per_row, side, _ = block_tiles.shape
    vmem = pl.BlockSpec(memory_space=pltpu.VMEM)
    smem = pl.BlockSpec(memory_space=pltpu.SMEM)
    out = jax.ShapeDtypeStruct((rows, output_columns.shape[1], side, side), jnp.bfloat16)
    tile_rows = lambda count: pltpu.VMEM((count, per_row, side, side), jnp.bfloat16)
    columns, outs = tile_columns.T, output_columns.T

    def dense():
        return pl.pallas_call(
            functools.partial(dense_kernel, groups, members),
            out_shape=out,
            in_specs=[smem, smem, vmem],
            out_specs=vmem,
            scratch_shapes=[
                tile_rows(n),
                tile_rows(n),
                tile_rows(rows),
                pltpu.SemaphoreType.DMA((n,)),
                pltpu.SemaphoreType.DMA((n,)),
                pltpu.SemaphoreType.DMA,
                pltpu.SemaphoreType.DMA,
            ],
            compiler_params=params(0),
        )(columns, outs, block_tiles)

    lines = members // PLANE
    crowd = groups * PLANE
    held = crowd * rows * per_row + (lines - 1) * CAP_B
    fits = groups == 2 and members == lines * PLANE and lines <= 4 and per_row == 2
    fits = fits and tile_columns.shape[0] == 256 and side % (16 * crowd) == 0 and held <= 256
    if not fits:
        return dense()
    piece = side // crowd
    pieces = lambda *lead: pltpu.VMEM((*lead, piece, side), jnp.bfloat16)
    dma = pltpu.SemaphoreType.DMA
    compact, over = pl.pallas_call(
        functools.partial(compact_kernel, groups, members),
        out_shape=(out, jax.ShapeDtypeStruct((1,), jnp.int32)),
        in_specs=[smem, smem, vmem, pl.BlockSpec(memory_space=pl.ANY)],
        out_specs=(vmem, smem),
        scratch_shapes=[
            pltpu.VMEM(block_tiles.shape, jnp.bfloat16),
            pieces(crowd, rows, per_row),
            pieces(held),
            pieces(lines - 1, CAP_B),
            pieces(lines - 1, CAP_B),
            pieces(crowd, CAP_C),
            pieces(crowd, CAP_C),
            pltpu.VMEM((8, 128), jnp.int32),
            pltpu.SMEM((8, 128), jnp.int32),
            dma,
            dma,
            dma((crowd,)),
            dma((crowd,)),
            dma((3 * (lines - 1),)),
            dma((3 * (lines - 1),)),
            dma((2 * crowd,)),
            dma((2 * crowd,)),
        ],
        compiler_params=params(1),
    )(columns, outs, columns, block_tiles)
    return lax.cond(over[0] > 0, dense, lambda: compact)


def solution(mesh):
    placed = (
        P(("grp", "row"), None, None, None),
        P(),
        P(("grp", "row"), None),
        P(("grp", "row"), None),
    )
    return jax.shard_map(
        shards,
        mesh=mesh,
        in_specs=placed,
        out_specs=P(("grp", "row"), None, None, None),
        check_vma=False,
    )
```

time: 43.4 us -> 34.1 us (0.79)
  Pallas kernels: 41.2 us -> 31.8 us
    pallas_call x1, Pallas kernels: 41.2 us -> 31.8 us  [shards(): pl.pallas_call(functools.partial(compact_kernel, groups, members), out_sh...]
where the time goes in v1:
time: 34.1 us; the launch traced here: 33.9 us
  Pallas kernels  31.8 us (93%)
  local copies, waits for them, and re-layouts  1.47 us (4%)
  between operations  0.59 us (2%)
    pallas_call x1, Pallas kernels, shards(): pl.pallas_call(functools.partial(compact_kernel, groups, members), out_sh...  31.8 us
    unnamed x7, local copies, waits for them, and re-layouts  1.47 us

profile of v1, /device:TPU:0, one launch (start us, length us, event | category | flops | bytes accessed | tf_op | source)
XLA Modules:
  0.0 33.9 jit_solution(10506737585013764509)
XLA Ops:
  0.0 0.0 copy-start
  0.0 31.8 %shard_map.39 = (bf16[8,2,128,128]{3,2,1,0:T(8,128)(2,1)S(1)}, s32[1]{0:T(128)}) custom-call(s32[2,256]{1,0:T(2,128)} %bitcast.3, s32[2,8]{1,0:T(2,128)} %bitcast.6, s32[2,256]{1,0:T(2,128)} %bitcast.4, bf16[8,2,128,128]{3,2,1,0:T(8,128)(2,1)} %tiles_hbm.1), custom_call_target="tpu_custom_call" | custom-call | tf_op jit(solution)/shard_map/pallas_call | solution.py:531
  32.4 0.0 copy-start.1
  32.4 0.0 copy-start.2
  32.4 0.0 copy-done
  32.5 0.7 %copy-done.1 = s32[256,2]{0,1:T(2,128)S(1)} copy-done((s32[256,2]{0,1:T(2,128)S(1)}, s32[256,2]{0,1:T(2,128)}, u32[]{:S(2)}) %copy-start.1) | copy-done | bytes 2072
  33.1 0.0 copy-done.2
  33.1 0.8 %copy.9 = bf16[8,2,128,128]{3,2,1,0:T(8,128)(2,1)} copy(bf16[8,2,128,128]{3,2,1,0:T(8,128)(2,1)S(1)} %get-tuple-element.22) | data formatting | bytes 1048576
  (1 shorter events, 0.0 us)
Async XLA Ops:
  0.0 32.4 %copy-start = (bf16[8,2,128,128]{3,2,1,0:T(8,128)(2,1)S(1)}, bf16[8,2,128,128]{3,2,1,0:T(8,128)(2,1)}, u32[]{:S(2)}) copy-start(bf16[8,2,128,128]{3,2,1,0:T(8,128)(2,1)} %tiles_hbm.1) | copy-start | bytes 1572868
  32.4 0.7 %copy-start.1 = (s32[256,2]{0,1:T(2,128)S(1)}, s32[256,2]{0,1:T(2,128)}, u32[]{:S(2)}) copy-start(s32[256,2]{0,1:T(2,128)} %param.7) | copy-start | bytes 6148
  32.4 0.7 %copy-start.2 = (s32[8,2]{0,1:T(2,128)S(1)}, s32[8,2]{0,1:T(2,128)}, u32[]{:S(2)}) copy-start(s32[8,2]{0,1:T(2,128)} %param.8) | copy-start | bytes 196

commit v2 on v1

v2 whole, which is shorter than its diff:
```python
import functools

import jax
import jax.numpy as jnp
from jax import lax
from jax.experimental import pallas as pl
from jax.experimental.pallas import tpu as pltpu
from jax.sharding import PartitionSpec as P

MESH = pl.DeviceIdType.MESH
PLANE = 4
ROW_CUT = (1, 3)
CUT_B = (0, 2, 8, 22, 33)
PART_B = (8, 22)
CUT_C = (0, 3, 7, 17, 22)
SPAN = 40
TABLE = 16


def multiply(base, find, cols_ref, outs_ref, tiles_ref, rbuf, out_ref):
    rows, per_row, side, _ = tiles_ref.shape
    outs_row = outs_ref.shape[0]
    for i in range(rows):
        left = jnp.concatenate([tiles_ref[i, k] for k in range(per_row)], axis=1)
        stack = []
        for k in range(per_row):
            c = cols_ref[k, base + i]
            safe = jnp.maximum(c, 0)
            slot = find(safe // rows)
            line = []
            for p in range(outs_row):
                o = outs_ref[p, i]
                which = jnp.int32(0)
                hit = jnp.int32(0)
                for j in range(per_row):
                    same = cols_ref[j, safe] == o
                    which = jnp.where(same, j, which)
                    hit = jnp.where(same & (c >= 0), 1, hit)
                tile = rbuf[slot, which]
                line.append(tile * hit.astype(jnp.float32).astype(jnp.bfloat16))
            stack.append(jnp.concatenate(line, axis=1))
        right = jnp.concatenate(stack, axis=0)
        prod = jnp.dot(left, right, preferred_element_type=jnp.float32).astype(jnp.bfloat16)
        for p in range(outs_row):
            out_ref[i, p] = prod[:, p * side : (p + 1) * side]


def dense_kernel(
    groups, members, cols_ref, outs_ref, tiles_ref, out_ref,
    sbuf, rbuf, mbuf, send_sem, recv_sem, mirror_send, mirror_recv,
):
    part = members // 2
    n = groups * part
    rows, per_row, side, _ = tiles_ref.shape
    grp, row = lax.axis_index("grp"), lax.axis_index("row")
    half, spot = row // part, lax.rem(row, part)
    me = grp * part + spot
    base = (grp * members + row) * rows
    mirror_row = (1 - half) * part + spot
    mirror = {"grp": grp, "row": mirror_row}
    mirror_base = (grp * members + mirror_row) * rows

    def place(s):
        u = lax.rem(me + s, n)
        return u // part, half * part + lax.rem(u, part)

    def target(s):
        g, r = place(s)
        return {"grp": g, "row": r}

    barrier = pltpu.get_barrier_semaphore()
    pl.semaphore_signal(barrier, inc=1, device_id=mirror, device_id_type=MESH)

    def greet(s, carry):
        pl.semaphore_signal(barrier, inc=1, device_id=target(s), device_id_type=MESH)
        return carry

    lax.fori_loop(1, n, greet, 0)

    def asked(s, start):
        g, r = place(s)
        first = (g * members + r) * rows
        t = jnp.int32(0)
        for i in range(rows):
            for k in range(per_row):
                c = cols_ref[k, first + i] - start
                t = jnp.where((c >= 0) & (c < rows), c, t)
        return t

    def copy(s, level):
        return pltpu.make_async_remote_copy(
            src_ref=sbuf.at[level * n + s],
            dst_ref=rbuf.at[level * n + s],
            send_sem=send_sem.at[level * n + s],
            recv_sem=recv_sem.at[level * n + s],
            device_id=target(s),
            device_id_type=MESH,
        )

    def pack(s, carry):
        sbuf[s] = tiles_ref[asked(s, base)]
        return carry

    lax.fori_loop(1, n, pack, 0)
    pl.semaphore_wait(barrier, n)
    across = pltpu.make_async_remote_copy(
        src_ref=tiles_ref,
        dst_ref=mbuf,
        send_sem=mirror_send,
        recv_sem=mirror_recv,
        device_id=mirror,
        device_id_type=MESH,
    )
    across.start()

    def send(s, carry):
        copy(s, 0).start()
        return carry

    lax.fori_loop(1, n, send, 0)
    rbuf[0] = tiles_ref[asked(0, base)]
    across.wait()

    def relay(s, carry):
        sbuf[n + s] = mbuf[asked(s, mirror_base)]
        return carry

    lax.fori_loop(1, n, relay, 0)

    def forward(s, carry):
        copy(s, 1).start()
        return carry

    lax.fori_loop(1, n, forward, 0)
    rbuf[n] = mbuf[asked(0, mirror_base)]

    def land(s, carry):
        copy(s, 0).wait()
        copy(s, 1).wait()
        return carry

    lax.fori_loop(1, n, land, 0)

    def find(owner):
        owner_row = lax.rem(owner, members)
        spot_of = owner // members * part + lax.rem(owner_row, part)
        return lax.rem(me - spot_of + n, n) + jnp.where(owner_row // part == half, 0, n)

    multiply(base, find, cols_ref, outs_ref, tiles_ref, rbuf, out_ref)


def same(lane, rows, groups, members):
    device = lane // rows
    inner = lax.rem(device, members)
    spot = lax.rem(inner, PLANE)
    return device // members, inner // PLANE, spot // 2, lax.rem(spot, 2)


def ones(mask):
    return jnp.where(mask, 1.0, 0.0)


def across(a, b):
    dims = (((1,), (1,)), ((), ()))
    return lax.dot_general(
        a.astype(jnp.bfloat16), b.astype(jnp.bfloat16), dims, preferred_element_type=jnp.float32
    )


def iota(shape, axis):
    return lax.broadcasted_iota(jnp.int32, shape, axis)


def steps(value, bounds):
    return sum((value >= b).astype(jnp.int32) for b in bounds)


def named_rows(cols, here, rows, groups, members):
    g, z, y, x = here
    lines = members // PLANE
    crowd = groups * PLANE
    total = cols.shape[1]
    devices = groups * members
    count = devices + 8
    query = iota((count, total), 0)
    lane = iota((count, total), 1)
    og, oz, oy, ox = same(lane, rows, groups, members)
    rel = PLANE * lax.rem(og + g, 2) + 2 * lax.rem(oy + y, 2) + lax.rem(ox + x, 2)
    up = lax.rem(oz - z + lines, lines)
    alone = (query < devices) & (up == query // crowd) & (rel == lax.rem(query, crowd))
    plane = up == query - devices
    group = ones(alone | plane)
    index = iota((total, total), 0)
    hits = jnp.zeros((count, total), jnp.float32)
    for k in range(cols.shape[0]):
        hits = hits + across(group, ones(index == cols[k : k + 1]))
    return ones(hits > 0.5)


def ranked(stack, cols, upper):
    masks, ranks = [], []
    before = jnp.zeros((stack.shape[0], 1), jnp.float32)
    for j in range(cols.shape[0]):
        m = stack * ones(cols[j : j + 1] >= 0)
        ranks.append(across(m, upper) + before)
        masks.append(m)
        before = before + jnp.sum(m, axis=1, keepdims=True)
    return masks, ranks, before


def slots(held, first, stride, bounds):
    masks, ranks, sums = held
    start = jnp.zeros((8, 1), jnp.float32)
    used, at = [0.0 for _ in masks], [0.0 for _ in masks]
    for k, bound in enumerate(bounds):
        b = 8 * (first + k * stride)
        start = jnp.maximum(start, float(bound))
        for j in range(len(masks)):
            m = masks[j][b : b + 8]
            used[j] = used[j] + m
            at[j] = at[j] + m * (start + ranks[j][b : b + 8])
        start = start + sums[b : b + 8]
    return used, at, start


def triangle(total):
    return ones(iota((total, total), 0) > iota((total, total), 1))


def tables(cols, named, here, rows, groups, members):
    g, z, y, x = here
    lines = members // PLANE
    crowd = groups * PLANE
    devices = groups * members
    total = cols.shape[1]
    per = cols.shape[0]
    lane = iota((8, total), 1)
    sub = iota((8, total), 0)
    og, oz, oy, ox = same(lane, rows, groups, members)
    rel = PLANE * lax.rem(og + g, 2) + 2 * lax.rem(oy + y, 2) + lax.rem(ox + x, 2)
    item = lax.rem(lane, rows)
    lev = steps(item, ROW_CUT)
    local = oz == z
    back = lax.rem(z - oz + lines, lines)
    planes = named[devices : devices + 8]
    mine = jnp.broadcast_to(planes[0:1], (8, total))
    near = named[:crowd]
    upper = triangle(total)
    classes = range(len(ROW_CUT) + 1)
    sends = [planes * ones(local & (lev == k)) for k in classes]
    takes = [mine * ones((back == sub) & (lev == k)) for k in classes]
    held = ranked(jnp.concatenate(sends + takes, axis=0), cols, upper)
    firsts = CUT_B[: len(classes)]
    send_used, send_at, _ = slots(held, 0, 1, firsts)
    take_used, take_at, _ = slots(held, len(classes), 1, firsts)
    arena = crowd * rows * per
    cap_b, cap_c = CUT_B[-1], CUT_C[-1]
    home = [(rel * (rows * per) + item * per + j).astype(jnp.float32) for j in range(per)]
    offset = (arena + (sub - 1) * cap_b).astype(jnp.float32)
    arrived, mids = [], [[] for _ in CUT_C[:-1]]
    for j in range(per):
        spot = jnp.sum(take_used[j] * take_at[j], axis=0, keepdims=True)
        far = jnp.sum(take_used[j] * (offset + take_at[j]), axis=0, keepdims=True)
        arrived.append(jnp.where(local, home[j], jnp.broadcast_to(far, (8, total))))
        part = jnp.where(local, 0, 1 + steps(jnp.broadcast_to(spot, (8, total)), PART_B))
        for c in range(len(mids)):
            mids[c].append(near * ones(part == c))

    def stacked(j):
        return jnp.concatenate([m[j] for m in mids], axis=0)

    masks, ranks = [], []
    before = jnp.zeros((8 * len(mids), 1), jnp.float32)
    for j in range(per):
        m = stacked(j) * ones(cols[j : j + 1] >= 0)
        ranks.append(across(m, upper) + before)
        masks.append(m)
        before = before + jnp.sum(m, axis=1, keepdims=True)
    mid_used, mid_at, _ = slots((masks, ranks, before), 0, 1, CUT_C[:-1])

    def sources(used, at, address, count):
        out = jnp.zeros((8, SPAN * count), jnp.float32)
        slot = iota((SPAN, total), 0)
        for j in range(per):
            spot = jnp.where(used[j] > 0.5, at[j], -1.0).astype(jnp.int32)
            hot = jnp.concatenate([ones(slot == spot[q : q + 1]) for q in range(count)], axis=0)
            out = out + across(address[j], hot)
        return jnp.clip(out.astype(jnp.int32), 0, arena + (lines - 1) * cap_b - 1)

    b_list = sources(send_used, send_at, home, lines)
    c_list = sources(mid_used, mid_at, arrived, crowd)
    final = [jnp.clip(mid_at[j][0:1].astype(jnp.int32), 0, cap_c - 1) for j in range(per)]
    lines_out = []
    for block in [b_list[0:1], c_list[0:1]] + final:
        width = block.shape[1]
        if width % 128:
            block = jnp.concatenate([block, jnp.zeros((1, -width % 128), jnp.int32)], axis=1)
        for h in range(-(-width // 128)):
            lines_out.append(block[:, 128 * h : 128 * h + 128])
    lines_out.append(jnp.zeros((TABLE - len(lines_out), 128), jnp.int32))
    return jnp.concatenate(lines_out, axis=0)


def overflow(cols, named, here, rows, groups, members):
    g, z, y, x = here
    lines = members // PLANE
    crowd = groups * PLANE
    devices = groups * members
    total = cols.shape[1]
    per = cols.shape[0]
    lane = iota((8, total), 1)
    oz = lax.rem(lane // rows, members) // PLANE
    up = lax.rem(oz - z + lines, lines)
    lev = steps(lax.rem(lane, rows), ROW_CUT)
    planes = named[devices : devices + 8]
    classes = range(len(ROW_CUT) + 1)
    stack = [planes * ones((up == s) & (lev == k)) for k in classes for s in range(lines)]
    held = ranked(jnp.concatenate(stack, axis=0), cols, triangle(total))
    sub = iota((8, 1), 0)
    worst = jnp.zeros((8, 1), jnp.float32)
    at = [0.0 for _ in range(per)]
    for s in range(lines):
        _, spot, end = slots(held, s, lines, CUT_B[: len(classes)])
        worst = jnp.maximum(worst, jnp.where((sub < lines) & (sub != s), end - CUT_B[-1], 0.0))
        for j in range(per):
            at[j] = at[j] + spot[j]
    for q in range(lines):
        near = named[crowd * q : crowd * (q + 1)]
        sums = [jnp.zeros((8, 1), jnp.float32) for _ in CUT_C[:-1]]
        for j in range(per):
            load = near * ones(cols[j : j + 1] >= 0)
            part = jnp.where(up == q, 0, 1 + steps(jnp.broadcast_to(at[j][q : q + 1], (8, total)), PART_B))
            for c in range(len(sums)):
                sums[c] = sums[c] + jnp.sum(load * ones(part == c), axis=1, keepdims=True)
        end = jnp.zeros((8, 1), jnp.float32)
        for bound, n in zip(CUT_C, sums):
            end = jnp.maximum(end, float(bound)) + n
        worst = jnp.maximum(worst, end - CUT_C[-1])
    return jnp.max(worst).astype(jnp.int32)


def compact_kernel(
    groups, members, cols_hbm, outs_hbm, tiles_hbm, out_ref, over_ref,
    cols_ref, outs_ref, cols_vec, tiles, parts, arena, b_send, b_recv, c_send, c_recv,
    tab_vec, tab, load_sem, tab_sem, a_out, a_in, b_out, b_in, c_out, c_in,
):
    rows, per, side, _ = tiles.shape
    lines = members // PLANE
    crowd = groups * PLANE
    piece = side // crowd
    g, row = lax.axis_index("grp"), lax.axis_index("row")
    z, spot = row // PLANE, lax.rem(row, PLANE)
    y, x = spot // 2, lax.rem(spot, 2)
    here = (g, z, y, x)
    base = (g * members + row) * rows
    me = g * PLANE + spot
    cuts_a = (0,) + ROW_CUT + (rows,)
    stages = len(cuts_a) - 1
    cap_b = CUT_B[-1]
    chunks_b, chunks_c = len(CUT_B) - 1, len(CUT_C) - 1

    def near_device(u):
        dg, dy, dx = u // PLANE, u // 2 % 2, u % 2
        ns = 2 * lax.rem(y + dy, 2) + lax.rem(x + dx, 2)
        return {"grp": lax.rem(g + dg, 2), "row": z * PLANE + ns}

    def line_device(dz):
        return {"grp": g, "row": lax.rem(z + dz, lines) * PLANE + spot}

    barrier = pltpu.get_barrier_semaphore()
    for dz in range(1, lines):
        pl.semaphore_signal(barrier, inc=1, device_id=line_device(dz), device_id_type=MESH)
    for u in range(crowd - 1, 0, -1):
        pl.semaphore_signal(barrier, inc=1, device_id=near_device(u), device_id_type=MESH)
    loads = [
        pltpu.make_async_copy(cols_hbm, cols_vec, load_sem.at[0]),
        pltpu.make_async_copy(tiles_hbm, tiles, load_sem.at[1]),
        pltpu.make_async_copy(cols_hbm, cols_ref, load_sem.at[2]),
        pltpu.make_async_copy(outs_hbm, outs_ref, load_sem.at[3]),
    ]
    for load in loads:
        load.start()
    loads[1].wait()
    pl.semaphore_wait(barrier, lines - 1 + crowd - 1)

    def a_copy(u, k):
        there = near_device(u)
        start = pl.multiple_of((there["grp"] * PLANE + lax.rem(there["row"], PLANE)) * piece, piece)
        span = pl.ds(cuts_a[k], cuts_a[k + 1] - cuts_a[k])
        return pltpu.make_async_remote_copy(
            src_ref=tiles.at[span, :, pl.ds(start, piece), :],
            dst_ref=parts.at[u, span],
            send_sem=a_out.at[stages * u + k],
            recv_sem=a_in.at[stages * u + k],
            device_id=there,
            device_id_type=MESH,
        )

    order = [3, 7, 1, 2, 5, 6, 4]
    for k in range(stages):
        for u in order:
            a_copy(u, k).start()

    loads[0].wait()
    cols = cols_vec[...]
    named = named_rows(cols, here, rows, groups, members)
    tab_vec[...] = tables(cols, named, here, rows, groups, members)
    move = pltpu.make_async_copy(tab_vec, tab, tab_sem)
    move.start()
    for load in loads[2:]:
        load.wait()
    mine = pl.multiple_of(me * piece, piece)
    for i in range(rows):
        for j in range(per):
            arena[i * per + j] = tiles[i, j, pl.ds(mine, piece), :]
    move.wait()

    def pick(options):
        value = jnp.int32(options[0])
        for at, option in enumerate(options[1:]):
            value = jnp.where(z == at + 1, option, value)
        return value

    far_first = [pick((3, 2, 2, 1)), pick((2, 1, 3, 2)), pick((1, 3, 1, 3))]

    def b_copy(k, dz):
        span = pl.ds(CUT_B[k], CUT_B[k + 1] - CUT_B[k])
        return pltpu.make_async_remote_copy(
            src_ref=b_send.at[dz - 1, span],
            dst_ref=b_recv.at[dz - 1, span],
            send_sem=b_out.at[chunks_b * (dz - 1) + k],
            recv_sem=b_in.at[chunks_b * (dz - 1) + k],
            device_id=line_device(dz),
            device_id_type=MESH,
        )

    def c_copy(k, u):
        span = pl.ds(CUT_C[k], CUT_C[k + 1] - CUT_C[k])
        return pltpu.make_async_remote_copy(
            src_ref=c_send.at[u, span],
            dst_ref=c_recv.at[u, span],
            send_sem=c_out.at[chunks_c * u + k],
            recv_sem=c_in.at[chunks_c * u + k],
            device_id=near_device(u),
            device_id_type=MESH,
        )

    wide_b, wide_c = -(-lines * SPAN // 128), -(-crowd * SPAN // 128)

    def entry(first, at):
        return tab[first + at // 128, at % 128]

    def push_b(k):
        for dz in range(1, lines):
            for q in range(CUT_B[k], CUT_B[k + 1]):
                b_send[dz - 1, q] = arena[entry(0, SPAN * dz + q)]
        for dz in far_first:
            b_copy(k, dz).start()

    def push_c(k):
        for u in order + [0]:
            for q in range(CUT_C[k], CUT_C[k + 1]):
                tile = arena[entry(wide_b, SPAN * u + q)]
                if u:
                    c_send[u, q] = tile
                else:
                    c_recv[0, q] = tile
        for core in range(groups):
            side_of = PLANE * lax.rem(core - g + groups, groups)
            for at in (3, 1, 2):
                c_copy(k, side_of + at).start()
        c_copy(k, PLANE).start()

    for k in range(stages):
        for u in order:
            a_copy(u, k).wait_recv()
            for i in range(cuts_a[k], cuts_a[k + 1]):
                for j in range(per):
                    arena[(u * rows + i) * per + j] = parts[u, i, j]
        push_b(k)
    for k in range(stages, chunks_b):
        push_b(k)
    push_c(0)
    over_ref[0] = overflow(cols, named, here, rows, groups, members)
    held = crowd * rows * per
    sent = 1
    for k in range(chunks_b):
        for dz in range(1, lines):
            b_copy(k, dz).wait_recv()
            for q in range(CUT_B[k], CUT_B[k + 1]):
                arena[held + (dz - 1) * cap_b + q] = b_recv[dz - 1, q]
        if CUT_B[k + 1] in PART_B or k == chunks_b - 1:
            push_c(sent)
            sent += 1

    sources = []
    for piece_of in range(crowd):
        pg, ps = piece_of // PLANE, piece_of % PLANE
        dy, dx = lax.rem(ps // 2 + y, 2), lax.rem(ps % 2 + x, 2)
        sources.append(PLANE * lax.rem(pg + g, 2) + 2 * dy + dx)
    for k in range(chunks_c):
        for u in order:
            c_copy(k, u).wait_recv()

    outs_row = outs_ref.shape[0]
    wide = cols_ref.shape[1] // 128
    for i in range(rows):
        left = jnp.concatenate([tiles[i, k] for k in range(per)], axis=1)
        stack = []
        for k in range(per):
            c = cols_ref[k, base + i]
            safe = jnp.maximum(c, 0)
            line = []
            for p in range(outs_row):
                o = outs_ref[p, i]
                which = jnp.int32(0)
                hit = jnp.int32(0)
                for j in range(per):
                    match = cols_ref[j, safe] == o
                    which = jnp.where(match, j, which)
                    hit = jnp.where(match & (c >= 0), 1, hit)
                slot = tab[wide_b + wide_c + wide * which + safe // 128, lax.rem(safe, 128)]
                tile = jnp.concatenate([c_recv[s, slot] for s in sources], axis=0)
                line.append(tile * hit.astype(jnp.float32).astype(jnp.bfloat16))
            stack.append(jnp.concatenate(line, axis=1))
        right = jnp.concatenate(stack, axis=0)
        prod = jnp.dot(left, right, preferred_element_type=jnp.float32).astype(jnp.bfloat16)
        for p in range(outs_row):
            out_ref[i, p] = prod[:, p * side : (p + 1) * side]

    for u in order:
        for k in range(stages):
            a_copy(u, k).wait_send()
        for k in range(chunks_c):
            c_copy(k, u).wait_send()
    for dz in range(1, lines):
        for k in range(chunks_b):
            b_copy(k, dz).wait_send()


def params(identity):
    return pltpu.CompilerParams(
        collective_id=identity, has_side_effects=True, vmem_limit_bytes=56 * 1024 * 1024
    )


def shards(block_tiles, tile_columns, requests, output_columns):
    groups = lax.axis_size("grp")
    members = lax.axis_size("row")
    n = groups * members
    rows, per_row, side, _ = block_tiles.shape
    vmem = pl.BlockSpec(memory_space=pltpu.VMEM)
    smem = pl.BlockSpec(memory_space=pltpu.SMEM)
    out = jax.ShapeDtypeStruct((rows, output_columns.shape[1], side, side), jnp.bfloat16)
    tile_rows = lambda count: pltpu.VMEM((count, per_row, side, side), jnp.bfloat16)
    columns, outs = tile_columns.T, output_columns.T

    def dense():
        return pl.pallas_call(
            functools.partial(dense_kernel, groups, members),
            out_shape=out,
            in_specs=[smem, smem, vmem],
            out_specs=vmem,
            scratch_shapes=[
                tile_rows(n),
                tile_rows(n),
                tile_rows(rows),
                pltpu.SemaphoreType.DMA((n,)),
                pltpu.SemaphoreType.DMA((n,)),
                pltpu.SemaphoreType.DMA,
                pltpu.SemaphoreType.DMA,
            ],
            compiler_params=params(0),
        )(columns, outs, block_tiles)

    lines = members // PLANE
    crowd = groups * PLANE
    cap_b, cap_c = CUT_B[-1], CUT_C[-1]
    held = crowd * rows * per_row + (lines - 1) * cap_b
    fits = groups == 2 and members == 4 * PLANE and per_row == 2 and rows > ROW_CUT[-1]
    fits = fits and tile_columns.shape[0] % 128 == 0 and side % (16 * crowd) == 0 and held <= 256
    if not fits:
        return dense()
    piece = side // crowd
    pieces = lambda *lead: pltpu.VMEM((*lead, piece, side), jnp.bfloat16)
    dma = pltpu.SemaphoreType.DMA
    hbm = pl.BlockSpec(memory_space=pl.ANY)
    stages, chunks_b, chunks_c = len(ROW_CUT) + 1, len(CUT_B) - 1, len(CUT_C) - 1
    compact, over = pl.pallas_call(
        functools.partial(compact_kernel, groups, members),
        out_shape=(out, jax.ShapeDtypeStruct((1,), jnp.int32)),
        in_specs=[hbm, hbm, hbm],
        out_specs=(vmem, smem),
        scratch_shapes=[
            pltpu.SMEM(columns.shape, jnp.int32),
            pltpu.SMEM(outs.shape, jnp.int32),
            pltpu.VMEM(columns.shape, jnp.int32),
            pltpu.VMEM(block_tiles.shape, jnp.bfloat16),
            pieces(crowd, rows, per_row),
            pieces(held),
            pieces(lines - 1, cap_b),
            pieces(lines - 1, cap_b),
            pieces(crowd, cap_c),
            pieces(crowd, cap_c),
            pltpu.VMEM((TABLE, 128), jnp.int32),
            pltpu.SMEM((TABLE, 128), jnp.int32),
            dma((4,)),
            dma,
            dma((stages * crowd,)),
            dma((stages * crowd,)),
            dma((chunks_b * (lines - 1),)),
            dma((chunks_b * (lines - 1),)),
            dma((chunks_c * crowd,)),
            dma((chunks_c * crowd,)),
        ],
        compiler_params=params(1),
    )(columns, outs, block_tiles)
    return lax.cond(over[0] > 0, dense, lambda: compact)


def solution(mesh):
    placed = (
        P(("grp", "row"), None, None, None),
        P(),
        P(("grp", "row"), None),
        P(("grp", "row"), None),
    )
    return jax.shard_map(
        shards,
        mesh=mesh,
        in_specs=placed,
        out_specs=P(("grp", "row"), None, None, None),
        check_vma=False,
    )
```

time: 34.1 us -> 31.4 us (0.921)
  Pallas kernels: 31.8 us -> 29 us
    pallas_call x1, Pallas kernels: 31.8 us -> 29 us  [shards(): pl.pallas_call(functools.partial(compact_kernel, groups, members), out_sh...]
where the time goes in v2:
time: 31.4 us; the launch traced here: 31.1 us
  Pallas kernels  29 us (92%)
  local copies, waits for them, and re-layouts  1.47 us (5%)
  between operations  0.59 us (2%)
    pallas_call x1, Pallas kernels, shards(): pl.pallas_call(functools.partial(compact_kernel, groups, members), out_sh...  29 us
    unnamed x7, local copies, waits for them, and re-layouts  1.47 us

profile of v2, /device:TPU:0, one launch (start us, length us, event | category | flops | bytes accessed | tf_op | source)
XLA Modules:
  0.0 31.1 jit_solution(10729314939090126767)
XLA Ops:
  0.0 0.0 copy-start
  0.0 29.0 %shard_map.39 = (bf16[8,2,128,128]{3,2,1,0:T(8,128)(2,1)S(1)}, s32[1]{0:T(128)}) custom-call(s32[2,256]{1,0:T(2,128)} %bitcast.3, s32[2,8]{1,0:T(2,128)} %bitcast.5, bf16[8,2,128,128]{3,2,1,0:T(8,128)(2,1)} %tiles_hbm.1), custom_call_target="tpu_custom_call" | custom-call | tf_op jit(solution)/shard_map/pallas_call | solution.py:589
  29.6 0.0 copy-start.1
  29.6 0.0 copy-start.2
  29.6 0.0 copy-done
  29.6 0.7 %copy-done.1 = s32[256,2]{0,1:T(2,128)S(1)} copy-done((s32[256,2]{0,1:T(2,128)S(1)}, s32[256,2]{0,1:T(2,128)}, u32[]{:S(2)}) %copy-start.1) | copy-done | bytes 2072
  30.3 0.0 copy-done.2
  30.3 0.8 %copy.9 = bf16[8,2,128,128]{3,2,1,0:T(8,128)(2,1)} copy(bf16[8,2,128,128]{3,2,1,0:T(8,128)(2,1)S(1)} %get-tuple-element.22) | data formatting | bytes 1048576
  (1 shorter events, 0.0 us)
Async XLA Ops:
  0.0 29.6 %copy-start = (bf16[8,2,128,128]{3,2,1,0:T(8,128)(2,1)S(1)}, bf16[8,2,128,128]{3,2,1,0:T(8,128)(2,1)}, u32[]{:S(2)}) copy-start(bf16[8,2,128,128]{3,2,1,0:T(8,128)(2,1)} %tiles_hbm.1) | copy-start | bytes 1572868
  29.6 0.7 %copy-start.1 = (s32[256,2]{0,1:T(2,128)S(1)}, s32[256,2]{0,1:T(2,128)}, u32[]{:S(2)}) copy-start(s32[256,2]{0,1:T(2,128)} %param.7) | copy-start | bytes 6148
  29.6 0.7 %copy-start.2 = (s32[8,2]{0,1:T(2,128)S(1)}, s32[8,2]{0,1:T(2,128)}, u32[]{:S(2)}) copy-start(s32[8,2]{0,1:T(2,128)} %param.8) | copy-start | bytes 196

commit v3 on v2

--- a/solution.py
+++ b/solution.py
@@ -9,10 +9,12 @@
 
 MESH = pl.DeviceIdType.MESH
 PLANE = 4
-ROW_CUT = (1, 3)
-CUT_B = (0, 2, 8, 22, 33)
-PART_B = (8, 22)
-CUT_C = (0, 3, 7, 17, 22)
+CUT_A = (0, 2, 6, 12)
+START_B = (0, 6, 20)
+CUT_B = (0, 6, 13, 20, 32)
+CLASS_B = (0, 1, 1, 2)
+PART_B = (13, 20)
+CUT_C = (0, 3, 10, 16, 21)
 SPAN = 40
 TABLE = 16
 
@@ -197,13 +199,11 @@
     return ones(hits > 0.5)
 
 
-def ranked(stack, cols, upper):
-    masks, ranks = [], []
-    before = jnp.zeros((stack.shape[0], 1), jnp.float32)
-    for j in range(cols.shape[0]):
-        m = stack * ones(cols[j : j + 1] >= 0)
+def ranked(masks, upper):
+    ranks = []
+    before = jnp.zeros((masks[0].shape[0], 1), jnp.float32)
+    for m in masks:
         ranks.append(across(m, upper) + before)
-        masks.append(m)
         before = before + jnp.sum(m, axis=1, keepdims=True)
     return masks, ranks, before
 
@@ -227,7 +227,40 @@
     return ones(iota((total, total), 0) > iota((total, total), 1))
 
 
-def tables(cols, named, here, rows, groups, members):
+def column(slot, spot, count):
+    hot = [ones(slot == spot[q : q + 1]) for q in range(count)]
+    return jnp.concatenate(hot, axis=0)
+
+
+def owned(cols, named, here, rows, groups, members):
+    devices = groups * members
+    total = cols.shape[1]
+    per = cols.shape[0]
+    wanted = ones(jnp.sum(named[devices : devices + 8], axis=0, keepdims=True) > 0.5)
+    masks = [jnp.broadcast_to(wanted * ones(cols[j : j + 1] >= 0), (8, total)) for j in range(per)]
+    a, b = iota((total, total), 0), iota((total, total), 1)
+    block = a // rows == b // rows
+    upper, whole = ones(block & (a > b)), ones(block)
+    ranks = []
+    before = jnp.zeros((8, total), jnp.float32)
+    for m in masks:
+        ranks.append(across(m, upper) + before)
+        before = before + across(m, whole)
+    lane = iota((8, total), 1)
+    og, oz, oy, ox = same(lane, rows, groups, members)
+    g, z, y, x = here
+    mine = (og == g) & (oz == z) & (oy == y) & (ox == x)
+    item = lax.rem(lane, rows)
+    picks = jnp.zeros((8, 128), jnp.float32)
+    slot = iota((128, total), 0)
+    for j in range(per):
+        spot = jnp.where(mine & (masks[j] > 0.5), ranks[j], -1.0).astype(jnp.int32)
+        picks = picks + across((item * per + j).astype(jnp.float32), column(slot, spot, 1))
+    picks = jnp.clip(picks.astype(jnp.int32), 0, rows * per - 1)
+    return ranks, before, picks
+
+
+def tables(cols, named, ranks_a, here, rows, groups, members):
     g, z, y, x = here
     lines = members // PLANE
     crowd = groups * PLANE
@@ -238,53 +271,44 @@
     sub = iota((8, total), 0)
     og, oz, oy, ox = same(lane, rows, groups, members)
     rel = PLANE * lax.rem(og + g, 2) + 2 * lax.rem(oy + y, 2) + lax.rem(ox + x, 2)
-    item = lax.rem(lane, rows)
-    lev = steps(item, ROW_CUT)
     local = oz == z
     back = lax.rem(z - oz + lines, lines)
     planes = named[devices : devices + 8]
     mine = jnp.broadcast_to(planes[0:1], (8, total))
     near = named[:crowd]
     upper = triangle(total)
-    classes = range(len(ROW_CUT) + 1)
-    sends = [planes * ones(local & (lev == k)) for k in classes]
-    takes = [mine * ones((back == sub) & (lev == k)) for k in classes]
-    held = ranked(jnp.concatenate(sends + takes, axis=0), cols, upper)
-    firsts = CUT_B[: len(classes)]
-    send_used, send_at, _ = slots(held, 0, 1, firsts)
-    take_used, take_at, _ = slots(held, len(classes), 1, firsts)
-    arena = crowd * rows * per
-    cap_b, cap_c = CUT_B[-1], CUT_C[-1]
-    home = [(rel * (rows * per) + item * per + j).astype(jnp.float32) for j in range(per)]
+    classes = range(len(START_B))
+    present = [ones(cols[j : j + 1] >= 0) for j in range(per)]
+    sends, takes = planes * ones(local), mine * ones(back == sub)
+    stacks = []
+    for j in range(per):
+        lev = steps(ranks_a[j], CUT_A[1:-1])
+        kept = [present[j] * ones(lev == k) for k in classes]
+        stacks.append(jnp.concatenate([sends * m for m in kept] + [takes * m for m in kept], axis=0))
+    held = ranked(stacks, upper)
+    send_used, send_at, _ = slots(held, 0, 1, START_B)
+    take_used, take_at, _ = slots(held, len(classes), 1, START_B)
+    cap_a, cap_b, cap_c = CUT_A[-1], CUT_B[-1], CUT_C[-1]
+    arena = crowd * cap_a
+    first = (rel * cap_a).astype(jnp.float32)
+    home = [first + jnp.minimum(ranks_a[j], cap_a - 1.0) for j in range(per)]
     offset = (arena + (sub - 1) * cap_b).astype(jnp.float32)
-    arrived, mids = [], [[] for _ in CUT_C[:-1]]
+    arrived, mids = [], []
     for j in range(per):
         spot = jnp.sum(take_used[j] * take_at[j], axis=0, keepdims=True)
         far = jnp.sum(take_used[j] * (offset + take_at[j]), axis=0, keepdims=True)
         arrived.append(jnp.where(local, home[j], jnp.broadcast_to(far, (8, total))))
         part = jnp.where(local, 0, 1 + steps(jnp.broadcast_to(spot, (8, total)), PART_B))
-        for c in range(len(mids)):
-            mids[c].append(near * ones(part == c))
-
-    def stacked(j):
-        return jnp.concatenate([m[j] for m in mids], axis=0)
-
-    masks, ranks = [], []
-    before = jnp.zeros((8 * len(mids), 1), jnp.float32)
-    for j in range(per):
-        m = stacked(j) * ones(cols[j : j + 1] >= 0)
-        ranks.append(across(m, upper) + before)
-        masks.append(m)
-        before = before + jnp.sum(m, axis=1, keepdims=True)
-    mid_used, mid_at, _ = slots((masks, ranks, before), 0, 1, CUT_C[:-1])
+        kept = near * present[j]
+        mids.append(jnp.concatenate([kept * ones(part == c) for c in range(len(CUT_C) - 1)], axis=0))
+    mid_used, mid_at, _ = slots(ranked(mids, upper), 0, 1, CUT_C[:-1])
 
     def sources(used, at, address, count):
         out = jnp.zeros((8, SPAN * count), jnp.float32)
         slot = iota((SPAN, total), 0)
         for j in range(per):
             spot = jnp.where(used[j] > 0.5, at[j], -1.0).astype(jnp.int32)
-            hot = jnp.concatenate([ones(slot == spot[q : q + 1]) for q in range(count)], axis=0)
-            out = out + across(address[j], hot)
+            out = out + across(address[j], column(slot, spot, count))
         return jnp.clip(out.astype(jnp.int32), 0, arena + (lines - 1) * cap_b - 1)
 
     b_list = sources(send_used, send_at, home, lines)
@@ -301,7 +325,7 @@
     return jnp.concatenate(lines_out, axis=0)
 
 
-def overflow(cols, named, here, rows, groups, members):
+def overflow(cols, named, ranks_a, loads_a, here, rows, groups, members):
     g, z, y, x = here
     lines = members // PLANE
     crowd = groups * PLANE
@@ -311,16 +335,24 @@
     lane = iota((8, total), 1)
     oz = lax.rem(lane // rows, members) // PLANE
     up = lax.rem(oz - z + lines, lines)
-    lev = steps(lax.rem(lane, rows), ROW_CUT)
     planes = named[devices : devices + 8]
-    classes = range(len(ROW_CUT) + 1)
-    stack = [planes * ones((up == s) & (lev == k)) for k in classes for s in range(lines)]
-    held = ranked(jnp.concatenate(stack, axis=0), cols, triangle(total))
+    classes = range(len(START_B))
+    present = [ones(cols[j : j + 1] >= 0) for j in range(per)]
+    stacks = []
+    for j in range(per):
+        lev = steps(ranks_a[j], CUT_A[1:-1])
+        kept = planes * present[j]
+        stacks.append(
+            jnp.concatenate(
+                [kept * ones((up == s) & (lev == k)) for k in classes for s in range(lines)], axis=0
+            )
+        )
+    held = ranked(stacks, triangle(total))
     sub = iota((8, 1), 0)
-    worst = jnp.zeros((8, 1), jnp.float32)
+    worst = jnp.maximum(jnp.max(loads_a, axis=1, keepdims=True) - CUT_A[-1], 0.0)
     at = [0.0 for _ in range(per)]
     for s in range(lines):
-        _, spot, end = slots(held, s, lines, CUT_B[: len(classes)])
+        _, spot, end = slots(held, s, lines, START_B)
         worst = jnp.maximum(worst, jnp.where((sub < lines) & (sub != s), end - CUT_B[-1], 0.0))
         for j in range(per):
             at[j] = at[j] + spot[j]
@@ -328,8 +360,9 @@
         near = named[crowd * q : crowd * (q + 1)]
         sums = [jnp.zeros((8, 1), jnp.float32) for _ in CUT_C[:-1]]
         for j in range(per):
-            load = near * ones(cols[j : j + 1] >= 0)
-            part = jnp.where(up == q, 0, 1 + steps(jnp.broadcast_to(at[j][q : q + 1], (8, total)), PART_B))
+            load = near * present[j]
+            spot = jnp.broadcast_to(at[j][q : q + 1], (8, total))
+            part = jnp.where(up == q, 0, 1 + steps(spot, PART_B))
             for c in range(len(sums)):
                 sums[c] = sums[c] + jnp.sum(load * ones(part == c), axis=1, keepdims=True)
         end = jnp.zeros((8, 1), jnp.float32)
@@ -341,8 +374,8 @@
 
 def compact_kernel(
     groups, members, cols_hbm, outs_hbm, tiles_hbm, out_ref, over_ref,
-    cols_ref, outs_ref, cols_vec, tiles, parts, arena, b_send, b_recv, c_send, c_recv,
-    tab_vec, tab, load_sem, tab_sem, a_out, a_in, b_out, b_in, c_out, c_in,
+    cols_ref, outs_ref, cols_vec, tiles, a_send, parts, arena, b_send, b_recv, c_send, c_recv,
+    own_vec, own, tab_vec, tab, load_sem, tab_sem, a_out, a_in, b_out, b_in, c_out, c_in,
 ):
     rows, per, side, _ = tiles.shape
     lines = members // PLANE
@@ -354,9 +387,7 @@
     here = (g, z, y, x)
     base = (g * members + row) * rows
     me = g * PLANE + spot
-    cuts_a = (0,) + ROW_CUT + (rows,)
-    stages = len(cuts_a) - 1
-    cap_b = CUT_B[-1]
+    stages, cap_a, cap_b = len(CUT_A) - 1, CUT_A[-1], CUT_B[-1]
     chunks_b, chunks_c = len(CUT_B) - 1, len(CUT_C) - 1
 
     def near_device(u):
@@ -380,15 +411,27 @@
     ]
     for load in loads:
         load.start()
-    loads[1].wait()
+    loads[0].wait()
+    cols = cols_vec[...]
+    named = named_rows(cols, here, rows, groups, members)
+    ranks_a, loads_a, picks = owned(cols, named, here, rows, groups, members)
+    own_vec[...] = picks
+    move = pltpu.make_async_copy(own_vec, own, tab_sem.at[0])
+    move.start()
+    for load in loads[1:]:
+        load.wait()
+    move.wait()
+    for q in range(cap_a):
+        pick = own[0, q]
+        a_send[q] = tiles[pick // per, lax.rem(pick, per)]
     pl.semaphore_wait(barrier, lines - 1 + crowd - 1)
 
     def a_copy(u, k):
         there = near_device(u)
         start = pl.multiple_of((there["grp"] * PLANE + lax.rem(there["row"], PLANE)) * piece, piece)
-        span = pl.ds(cuts_a[k], cuts_a[k + 1] - cuts_a[k])
+        span = pl.ds(CUT_A[k], CUT_A[k + 1] - CUT_A[k])
         return pltpu.make_async_remote_copy(
-            src_ref=tiles.at[span, :, pl.ds(start, piece), :],
+            src_ref=a_send.at[span, pl.ds(start, piece), :],
             dst_ref=parts.at[u, span],
             send_sem=a_out.at[stages * u + k],
             recv_sem=a_in.at[stages * u + k],
@@ -401,18 +444,12 @@
         for u in order:
             a_copy(u, k).start()
 
-    loads[0].wait()
-    cols = cols_vec[...]
-    named = named_rows(cols, here, rows, groups, members)
-    tab_vec[...] = tables(cols, named, here, rows, groups, members)
-    move = pltpu.make_async_copy(tab_vec, tab, tab_sem)
+    tab_vec[...] = tables(cols, named, ranks_a, here, rows, groups, members)
+    move = pltpu.make_async_copy(tab_vec, tab, tab_sem.at[1])
     move.start()
-    for load in loads[2:]:
-        load.wait()
     mine = pl.multiple_of(me * piece, piece)
-    for i in range(rows):
-        for j in range(per):
-            arena[i * per + j] = tiles[i, j, pl.ds(mine, piece), :]
+    for q in range(cap_a):
+        arena[q] = a_send[q, pl.ds(mine, piece), :]
     move.wait()
 
     def pick(options):
@@ -474,15 +511,14 @@
     for k in range(stages):
         for u in order:
             a_copy(u, k).wait_recv()
-            for i in range(cuts_a[k], cuts_a[k + 1]):
-                for j in range(per):
-                    arena[(u * rows + i) * per + j] = parts[u, i, j]
-        push_b(k)
-    for k in range(stages, chunks_b):
-        push_b(k)
+            for q in range(CUT_A[k], CUT_A[k + 1]):
+                arena[u * cap_a + q] = parts[u, q]
+        for part in range(chunks_b):
+            if CLASS_B[part] == k:
+                push_b(part)
     push_c(0)
-    over_ref[0] = overflow(cols, named, here, rows, groups, members)
-    held = crowd * rows * per
+    over_ref[0] = overflow(cols, named, ranks_a, loads_a, here, rows, groups, members)
+    held = crowd * cap_a
     sent = 1
     for k in range(chunks_b):
         for dz in range(1, lines):
@@ -576,8 +612,8 @@
     lines = members // PLANE
     crowd = groups * PLANE
     cap_b, cap_c = CUT_B[-1], CUT_C[-1]
-    held = crowd * rows * per_row + (lines - 1) * cap_b
-    fits = groups == 2 and members == 4 * PLANE and per_row == 2 and rows > ROW_CUT[-1]
+    held = crowd * CUT_A[-1] + (lines - 1) * cap_b
+    fits = groups == 2 and members == 4 * PLANE and per_row == 2 and CUT_A[-1] <= 128
     fits = fits and tile_columns.shape[0] % 128 == 0 and side % (16 * crowd) == 0 and held <= 256
     if not fits:
         return dense()
@@ -585,7 +621,7 @@
     pieces = lambda *lead: pltpu.VMEM((*lead, piece, side), jnp.bfloat16)
     dma = pltpu.SemaphoreType.DMA
     hbm = pl.BlockSpec(memory_space=pl.ANY)
-    stages, chunks_b, chunks_c = len(ROW_CUT) + 1, len(CUT_B) - 1, len(CUT_C) - 1
+    stages, chunks_b, chunks_c = len(CUT_A) - 1, len(CUT_B) - 1, len(CUT_C) - 1
     compact, over = pl.pallas_call(
         functools.partial(compact_kernel, groups, members),
         out_shape=(out, jax.ShapeDtypeStruct((1,), jnp.int32)),
@@ -596,16 +632,19 @@
             pltpu.SMEM(outs.shape, jnp.int32),
             pltpu.VMEM(columns.shape, jnp.int32),
             pltpu.VMEM(block_tiles.shape, jnp.bfloat16),
-            pieces(crowd, rows, per_row),
+            pltpu.VMEM((CUT_A[-1], side, side), jnp.bfloat16),
+            pieces(crowd, CUT_A[-1]),
             pieces(held),
             pieces(lines - 1, cap_b),
             pieces(lines - 1, cap_b),
             pieces(crowd, cap_c),
             pieces(crowd, cap_c),
+            pltpu.VMEM((8, 128), jnp.int32),
+            pltpu.SMEM((8, 128), jnp.int32),
             pltpu.VMEM((TABLE, 128), jnp.int32),
             pltpu.SMEM((TABLE, 128), jnp.int32),
             dma((4,)),
-            dma,
+            dma((2,)),
             dma((stages * crowd,)),
             dma((stages * crowd,)),
             dma((chunks_b * (lines - 1),)),

time: 31.4 us -> 30.2 us (0.962)
  Pallas kernels: 29 us -> 28 us
    pallas_call x1, Pallas kernels: 29 us -> 28 us  [shards(): pl.pallas_call(functools.partial(compact_kernel, groups, members), out_sh...]
where the time goes in v3:
time: 30.2 us; the launch traced here: 30 us
  Pallas kernels  28 us (93%)
  local copies, waits for them, and re-layouts  1.47 us (5%)
  between operations  0.59 us (2%)
    pallas_call x1, Pallas kernels, shards(): pl.pallas_call(functools.partial(compact_kernel, groups, members), out_sh...  28 us
    unnamed x7, local copies, waits for them, and re-layouts  1.47 us

profile of v3, /device:TPU:0, one launch (start us, length us, event | category | flops | bytes accessed | tf_op | source)
XLA Modules:
  0.0 30.0 jit_solution(17626591874898990707)
XLA Ops:
  0.0 0.0 copy-start
  0.0 28.0 %shard_map.39 = (bf16[8,2,128,128]{3,2,1,0:T(8,128)(2,1)S(1)}, s32[1]{0:T(128)}) custom-call(s32[2,256]{1,0:T(2,128)} %bitcast.3, s32[2,8]{1,0:T(2,128)} %bitcast.5, bf16[8,2,128,128]{3,2,1,0:T(8,128)(2,1)} %tiles_hbm.1), custom_call_target="tpu_custom_call" | custom-call | tf_op jit(solution)/shard_map/pallas_call | solution.py:625
  28.5 0.0 copy-start.1
  28.5 0.0 copy-start.2
  28.5 0.0 copy-done
  28.6 0.7 %copy-done.1 = s32[256,2]{0,1:T(2,128)S(1)} copy-done((s32[256,2]{0,1:T(2,128)S(1)}, s32[256,2]{0,1:T(2,128)}, u32[]{:S(2)}) %copy-start.1) | copy-done | bytes 2072
  29.2 0.0 copy-done.2
  29.2 0.8 %copy.9 = bf16[8,2,128,128]{3,2,1,0:T(8,128)(2,1)} copy(bf16[8,2,128,128]{3,2,1,0:T(8,128)(2,1)S(1)} %get-tuple-element.22) | data formatting | bytes 1048576
  (1 shorter events, 0.0 us)
Async XLA Ops:
  0.0 28.5 %copy-start = (bf16[8,2,128,128]{3,2,1,0:T(8,128)(2,1)S(1)}, bf16[8,2,128,128]{3,2,1,0:T(8,128)(2,1)}, u32[]{:S(2)}) copy-start(bf16[8,2,128,128]{3,2,1,0:T(8,128)(2,1)} %tiles_hbm.1) | copy-start | bytes 1572868
  28.5 0.7 %copy-start.1 = (s32[256,2]{0,1:T(2,128)S(1)}, s32[256,2]{0,1:T(2,128)}, u32[]{:S(2)}) copy-start(s32[256,2]{0,1:T(2,128)} %param.7) | copy-start | bytes 6148
  28.5 0.7 %copy-start.2 = (s32[8,2]{0,1:T(2,128)S(1)}, s32[8,2]{0,1:T(2,128)}, u32[]{:S(2)}) copy-start(s32[8,2]{0,1:T(2,128)} %param.8) | copy-start | bytes 196

commit v4 on v3

--- a/solution.py
+++ b/solution.py
@@ -373,8 +373,8 @@
 
 
 def compact_kernel(
-    groups, members, cols_hbm, outs_hbm, tiles_hbm, out_ref, over_ref,
-    cols_ref, outs_ref, cols_vec, tiles, a_send, parts, arena, b_send, b_recv, c_send, c_recv,
+    groups, members, cols_hbm, outs_hbm, tiles_hbm, out_ref, over_ref, cols_vec, outs_vec,
+    cols_ref, outs_ref, tiles, a_send, parts, arena, b_send, b_recv, c_send, c_recv,
     own_vec, own, tab_vec, tab, load_sem, tab_sem, a_out, a_in, b_out, b_in, c_out, c_in,
 ):
     rows, per, side, _ = tiles.shape
@@ -408,6 +408,7 @@
         pltpu.make_async_copy(tiles_hbm, tiles, load_sem.at[1]),
         pltpu.make_async_copy(cols_hbm, cols_ref, load_sem.at[2]),
         pltpu.make_async_copy(outs_hbm, outs_ref, load_sem.at[3]),
+        pltpu.make_async_copy(outs_hbm, outs_vec, load_sem.at[4]),
     ]
     for load in loads:
         load.start()
@@ -439,7 +440,7 @@
             device_id_type=MESH,
         )
 
-    order = [3, 7, 1, 2, 5, 6, 4]
+    order = [7, 3, 5, 6, 1, 2, 4]
     for k in range(stages):
         for u in order:
             a_copy(u, k).start()
@@ -534,19 +535,21 @@
         pg, ps = piece_of // PLANE, piece_of % PLANE
         dy, dx = lax.rem(ps // 2 + y, 2), lax.rem(ps % 2 + x, 2)
         sources.append(PLANE * lax.rem(pg + g, 2) + 2 * dy + dx)
-    for k in range(chunks_c):
-        for u in order:
-            c_copy(k, u).wait_recv()
-
+    for u in order:
+        for k in range(stages):
+            a_copy(u, k).wait_send()
+        for k in range(chunks_c):
+            c_copy(k, u).wait_send()
+    for dz in range(1, lines):
+        for k in range(chunks_b):
+            b_copy(k, dz).wait_send()
     outs_row = outs_ref.shape[0]
     wide = cols_ref.shape[1] // 128
+    picks = {}
     for i in range(rows):
-        left = jnp.concatenate([tiles[i, k] for k in range(per)], axis=1)
-        stack = []
         for k in range(per):
             c = cols_ref[k, base + i]
             safe = jnp.maximum(c, 0)
-            line = []
             for p in range(outs_row):
                 o = outs_ref[p, i]
                 which = jnp.int32(0)
@@ -556,6 +559,18 @@
                     which = jnp.where(match, j, which)
                     hit = jnp.where(match & (c >= 0), 1, hit)
                 slot = tab[wide_b + wide_c + wide * which + safe // 128, lax.rem(safe, 128)]
+                picks[i, k, p] = slot, hit
+    for k in range(chunks_c):
+        for u in order:
+            c_copy(k, u).wait_recv()
+
+    for i in range(rows):
+        left = jnp.concatenate([tiles[i, k] for k in range(per)], axis=1)
+        stack = []
+        for k in range(per):
+            line = []
+            for p in range(outs_row):
+                slot, hit = picks[i, k, p]
                 tile = jnp.concatenate([c_recv[s, slot] for s in sources], axis=0)
                 line.append(tile * hit.astype(jnp.float32).astype(jnp.bfloat16))
             stack.append(jnp.concatenate(line, axis=1))
@@ -563,15 +578,6 @@
         prod = jnp.dot(left, right, preferred_element_type=jnp.float32).astype(jnp.bfloat16)
         for p in range(outs_row):
             out_ref[i, p] = prod[:, p * side : (p + 1) * side]
-
-    for u in order:
-        for k in range(stages):
-            a_copy(u, k).wait_send()
-        for k in range(chunks_c):
-            c_copy(k, u).wait_send()
-    for dz in range(1, lines):
-        for k in range(chunks_b):
-            b_copy(k, dz).wait_send()
 
 
 def params(identity):
@@ -622,15 +628,15 @@
     dma = pltpu.SemaphoreType.DMA
     hbm = pl.BlockSpec(memory_space=pl.ANY)
     stages, chunks_b, chunks_c = len(CUT_A) - 1, len(CUT_B) - 1, len(CUT_C) - 1
-    compact, over = pl.pallas_call(
+    like = lambda array: jax.ShapeDtypeStruct(array.shape, array.dtype)
+    compact, over, columns, outs = pl.pallas_call(
         functools.partial(compact_kernel, groups, members),
-        out_shape=(out, jax.ShapeDtypeStruct((1,), jnp.int32)),
+        out_shape=(out, jax.ShapeDtypeStruct((1,), jnp.int32), like(columns), like(outs)),
         in_specs=[hbm, hbm, hbm],
-        out_specs=(vmem, smem),
+        out_specs=(vmem, smem, vmem, vmem),
         scratch_shapes=[
             pltpu.SMEM(columns.shape, jnp.int32),
             pltpu.SMEM(outs.shape, jnp.int32),
-            pltpu.VMEM(columns.shape, jnp.int32),
             pltpu.VMEM(block_tiles.shape, jnp.bfloat16),
             pltpu.VMEM((CUT_A[-1], side, side), jnp.bfloat16),
             pieces(crowd, CUT_A[-1]),
@@ -643,7 +649,7 @@
             pltpu.SMEM((8, 128), jnp.int32),
             pltpu.VMEM((TABLE, 128), jnp.int32),
             pltpu.SMEM((TABLE, 128), jnp.int32),
-            dma((4,)),
+            dma((5,)),
             dma((2,)),
             dma((stages * crowd,)),
             dma((stages * crowd,)),

time: 30.2 us -> 29 us (0.960)
  local copies, waits for them, and re-layouts: 1.47 us -> 0.8 us
  Pallas kernels: 28 us -> 27.4 us
    unnamed x7 -> x3, local copies, waits for them, and re-layouts: 1.47 us -> 0.8 us
    pallas_call x1, Pallas kernels: 28 us -> 27.4 us  [shards(): pl.pallas_call(functools.partial(compact_kernel, groups, members), out_sh...]
where the time goes in v4:
time: 29 us; the launch traced here: 28.9 us
  Pallas kernels  27.4 us (94%)
  local copies, waits for them, and re-layouts  0.8 us (3%)
  between operations  0.63 us (2%)
    pallas_call x1, Pallas kernels, shards(): pl.pallas_call(functools.partial(compact_kernel, groups, members), out_sh...  27.4 us
    unnamed x3, local copies, waits for them, and re-layouts  0.8 us

profile of v4, /device:TPU:0, one launch (start us, length us, event | category | flops | bytes accessed | tf_op | source)
XLA Modules:
  0.0 28.9 jit_solution(12188788131160571646)
XLA Ops:
  0.0 0.0 copy-start
  0.0 27.4 %shard_map.39 = (bf16[8,2,128,128]{3,2,1,0:T(8,128)(2,1)S(1)}, s32[1]{0:T(128)}, s32[2,256]{1,0:T(2,128)S(1)}, s32[2,8]{1,0:T(2,128)S(1)}) custom-call(s32[2,256]{1,0:T(2,128)} %bitcast.3, s32[2,8]{1,0:T(2,128)} %bitcast.4, bf16[8,2,128,128]{3,2,1,0:T(8,128)(2,1)} %tiles_hbm.1), custom_call_target="tpu_custom_call" | custom-call | tf_op jit(solution)/shard_map/pallas_call | solution.py:632
  28.0 0.0 copy-done
  28.1 0.8 %copy.9 = bf16[8,2,128,128]{3,2,1,0:T(8,128)(2,1)} copy(bf16[8,2,128,128]{3,2,1,0:T(8,128)(2,1)S(1)} %get-tuple-element.26) | data formatting | bytes 1048576
  (1 shorter events, 0.0 us)
Async XLA Ops:
  0.0 28.0 %copy-start = (bf16[8,2,128,128]{3,2,1,0:T(8,128)(2,1)S(1)}, bf16[8,2,128,128]{3,2,1,0:T(8,128)(2,1)}, u32[]{:S(2)}) copy-start(bf16[8,2,128,128]{3,2,1,0:T(8,128)(2,1)} %tiles_hbm.1) | copy-start | bytes 1572868

commit v5 on v4

--- a/solution.py
+++ b/solution.py
@@ -11,10 +11,10 @@
 PLANE = 4
 CUT_A = (0, 2, 6, 12)
 START_B = (0, 6, 20)
-CUT_B = (0, 6, 13, 20, 32)
-CLASS_B = (0, 1, 1, 2)
-PART_B = (13, 20)
-CUT_C = (0, 3, 10, 16, 21)
+CUT_B = (0, 6, 20, 32)
+CLASS_B = (0, 1, 2)
+PART_B = (6, 20)
+CUT_C = (0, 3, 7, 16, 21)
 SPAN = 40
 TABLE = 16
 

time: 29 us -> 28.7 us (0.990)
  Pallas kernels: 27.4 us -> 27.1 us
    pallas_call x1, Pallas kernels: 27.4 us -> 27.1 us  [shards(): pl.pallas_call(functools.partial(compact_kernel, groups, members), out_sh...]
where the time goes in v5:
time: 28.7 us; the launch traced here: 28.5 us
  Pallas kernels  27.1 us (94%)
  local copies, waits for them, and re-layouts  0.8 us (3%)
  between operations  0.63 us (2%)
    pallas_call x1, Pallas kernels, shards(): pl.pallas_call(functools.partial(compact_kernel, groups, members), out_sh...  27.1 us
    unnamed x3, local copies, waits for them, and re-layouts  0.8 us

profile of v5, /device:TPU:0, one launch (start us, length us, event | category | flops | bytes accessed | tf_op | source)
XLA Modules:
  0.0 28.5 jit_solution(14072991468463008338)
XLA Ops:
  0.0 0.0 copy-start
  0.0 27.1 %shard_map.39 = (bf16[8,2,128,128]{3,2,1,0:T(8,128)(2,1)S(1)}, s32[1]{0:T(128)}, s32[2,256]{1,0:T(2,128)S(1)}, s32[2,8]{1,0:T(2,128)S(1)}) custom-call(s32[2,256]{1,0:T(2,128)} %bitcast.3, s32[2,8]{1,0:T(2,128)} %bitcast.4, bf16[8,2,128,128]{3,2,1,0:T(8,128)(2,1)} %tiles_hbm.1), custom_call_target="tpu_custom_call" | custom-call | tf_op jit(solution)/shard_map/pallas_call | solution.py:632
  27.7 0.0 copy-done
  27.7 0.8 %copy.9 = bf16[8,2,128,128]{3,2,1,0:T(8,128)(2,1)} copy(bf16[8,2,128,128]{3,2,1,0:T(8,128)(2,1)S(1)} %get-tuple-element.26) | data formatting | bytes 1048576
  (1 shorter events, 0.0 us)
Async XLA Ops:
  0.0 27.7 %copy-start = (bf16[8,2,128,128]{3,2,1,0:T(8,128)(2,1)S(1)}, bf16[8,2,128,128]{3,2,1,0:T(8,128)(2,1)}, u32[]{:S(2)}) copy-start(bf16[8,2,128,128]{3,2,1,0:T(8,128)(2,1)} %tiles_hbm.1) | copy-start | bytes 1572868

commit v6 on v5

--- a/solution.py
+++ b/solution.py
@@ -14,7 +14,7 @@
 CUT_B = (0, 6, 20, 32)
 CLASS_B = (0, 1, 2)
 PART_B = (6, 20)
-CUT_C = (0, 3, 7, 16, 21)
+CUT_C = (0, 2, 6, 15, 20)
 SPAN = 40
 TABLE = 16
 
@@ -177,11 +177,10 @@
     return sum((value >= b).astype(jnp.int32) for b in bounds)
 
 
-def named_rows(cols, here, rows, groups, members):
+def grouping(total, here, rows, groups, members):
     g, z, y, x = here
     lines = members // PLANE
     crowd = groups * PLANE
-    total = cols.shape[1]
     devices = groups * members
     count = devices + 8
     query = iota((count, total), 0)
@@ -191,9 +190,19 @@
     up = lax.rem(oz - z + lines, lines)
     alone = (query < devices) & (up == query // crowd) & (rel == lax.rem(query, crowd))
     plane = up == query - devices
-    group = ones(alone | plane)
+    return ones(alone | plane).astype(jnp.bfloat16)
+
+
+def blocks(total, rows):
+    a, b = iota((total, total), 0), iota((total, total), 1)
+    block = a // rows == b // rows
+    return ones(block & (a > b)).astype(jnp.bfloat16), ones(block).astype(jnp.bfloat16)
+
+
+def named_rows(cols, group):
+    total = cols.shape[1]
     index = iota((total, total), 0)
-    hits = jnp.zeros((count, total), jnp.float32)
+    hits = jnp.zeros((group.shape[0], total), jnp.float32)
     for k in range(cols.shape[0]):
         hits = hits + across(group, ones(index == cols[k : k + 1]))
     return ones(hits > 0.5)
@@ -232,15 +241,12 @@
     return jnp.concatenate(hot, axis=0)
 
 
-def owned(cols, named, here, rows, groups, members):
+def owned(cols, named, upper, whole, here, rows, groups, members):
     devices = groups * members
     total = cols.shape[1]
     per = cols.shape[0]
     wanted = ones(jnp.sum(named[devices : devices + 8], axis=0, keepdims=True) > 0.5)
     masks = [jnp.broadcast_to(wanted * ones(cols[j : j + 1] >= 0), (8, total)) for j in range(per)]
-    a, b = iota((total, total), 0), iota((total, total), 1)
-    block = a // rows == b // rows
-    upper, whole = ones(block & (a > b)), ones(block)
     ranks = []
     before = jnp.zeros((8, total), jnp.float32)
     for m in masks:
@@ -412,10 +418,13 @@
     ]
     for load in loads:
         load.start()
+    total = cols_vec.shape[1]
+    group = grouping(total, here, rows, groups, members)
+    upper, whole = blocks(total, rows)
     loads[0].wait()
     cols = cols_vec[...]
-    named = named_rows(cols, here, rows, groups, members)
-    ranks_a, loads_a, picks = owned(cols, named, here, rows, groups, members)
+    named = named_rows(cols, group)
+    ranks_a, loads_a, picks = owned(cols, named, upper, whole, here, rows, groups, members)
     own_vec[...] = picks
     move = pltpu.make_async_copy(own_vec, own, tab_sem.at[0])
     move.start()
@@ -424,15 +433,17 @@
     move.wait()
     for q in range(cap_a):
         pick = own[0, q]
-        a_send[q] = tiles[pick // per, lax.rem(pick, per)]
+        tile = tiles[pick // per, lax.rem(pick, per)]
+        for part in range(crowd):
+            a_send[part, q] = tile[part * piece : part * piece + piece]
     pl.semaphore_wait(barrier, lines - 1 + crowd - 1)
 
     def a_copy(u, k):
         there = near_device(u)
-        start = pl.multiple_of((there["grp"] * PLANE + lax.rem(there["row"], PLANE)) * piece, piece)
+        part = there["grp"] * PLANE + lax.rem(there["row"], PLANE)
         span = pl.ds(CUT_A[k], CUT_A[k + 1] - CUT_A[k])
         return pltpu.make_async_remote_copy(
-            src_ref=a_send.at[span, pl.ds(start, piece), :],
+            src_ref=a_send.at[part, span],
             dst_ref=parts.at[u, span],
             send_sem=a_out.at[stages * u + k],
             recv_sem=a_in.at[stages * u + k],
@@ -448,9 +459,8 @@
     tab_vec[...] = tables(cols, named, ranks_a, here, rows, groups, members)
     move = pltpu.make_async_copy(tab_vec, tab, tab_sem.at[1])
     move.start()
-    mine = pl.multiple_of(me * piece, piece)
     for q in range(cap_a):
-        arena[q] = a_send[q, pl.ds(mine, piece), :]
+        arena[q] = a_send[me, q]
     move.wait()
 
     def pick(options):
@@ -638,7 +648,7 @@
             pltpu.SMEM(columns.shape, jnp.int32),
             pltpu.SMEM(outs.shape, jnp.int32),
             pltpu.VMEM(block_tiles.shape, jnp.bfloat16),
-            pltpu.VMEM((CUT_A[-1], side, side), jnp.bfloat16),
+            pieces(crowd, CUT_A[-1]),
             pieces(crowd, CUT_A[-1]),
             pieces(held),
             pieces(lines - 1, cap_b),

time: 28.7 us -> 28.7 us (level)
  no operation moved by 1% of the time
where the time goes in v6:
time: 28.7 us; the launch traced here: 28.5 us
  Pallas kernels  27.1 us (94%)
  local copies, waits for them, and re-layouts  0.8 us (3%)
  between operations  0.63 us (2%)
    pallas_call x1, Pallas kernels, shards(): pl.pallas_call(functools.partial(compact_kernel, groups, members), out_sh...  27.1 us
    unnamed x3, local copies, waits for them, and re-layouts  0.8 us

profile of v6, /device:TPU:0, one launch (start us, length us, event | category | flops | bytes accessed | tf_op | source)
XLA Modules:
  0.0 28.5 jit_solution(5736230300444794686)
XLA Ops:
  0.0 0.0 copy-start
  0.0 27.1 %shard_map.39 = (bf16[8,2,128,128]{3,2,1,0:T(8,128)(2,1)S(1)}, s32[1]{0:T(128)}, s32[2,256]{1,0:T(2,128)S(1)}, s32[2,8]{1,0:T(2,128)S(1)}) custom-call(s32[2,256]{1,0:T(2,128)} %bitcast.3, s32[2,8]{1,0:T(2,128)} %bitcast.4, bf16[8,2,128,128]{3,2,1,0:T(8,128)(2,1)} %tiles_hbm.1), custom_call_target="tpu_custom_call" | custom-call | tf_op jit(solution)/shard_map/pallas_call | solution.py:642
  27.7 0.0 copy-done
  27.7 0.8 %copy.9 = bf16[8,2,128,128]{3,2,1,0:T(8,128)(2,1)} copy(bf16[8,2,128,128]{3,2,1,0:T(8,128)(2,1)S(1)} %get-tuple-element.26) | data formatting | bytes 1048576
  (1 shorter events, 0.0 us)
Async XLA Ops:
  0.0 27.7 %copy-start = (bf16[8,2,128,128]{3,2,1,0:T(8,128)(2,1)S(1)}, bf16[8,2,128,128]{3,2,1,0:T(8,128)(2,1)}, u32[]{:S(2)}) copy-start(bf16[8,2,128,128]{3,2,1,0:T(8,128)(2,1)} %tiles_hbm.1) | copy-start | bytes 1572868
